TPU v7x, 32 devices: a whole 2x2x4 slice. The times are simulated.
32 devices in a mesh: gx: 4 (over y, core), gy: 8 (over z, x).
Axes of the slice: x: 2, y: 2, z: 4, core: 2. Of those that a mesh axis runs over, the one named last changes fastest.
Arguments:
- tokens: bfloat16 [4, 256, 6144], P('gx', None, 'gy'), may hold values from -6 to 6
- norm_gain: float32 [6144], replicated, may hold values from 0.1 to 1.9
- qkv_weight: bfloat16 [6144, 3, 4096], P('gx', None, 'gy'), may hold values from -0.078125 to 0.078125
- up_weight: bfloat16 [6144, 24576], P('gx', 'gy'), may hold values from -0.078125 to 0.078125
- query_gain: float32 [128], replicated, may hold values from 0.1 to 1.9
- key_gain: float32 [128], replicated, may hold values from 0.1 to 1.9
- out_weight: bfloat16 [4096, 6144], P('gy', 'gx'), may hold values from -0.09375 to 0.09375
- down_weight: bfloat16 [24576, 6144], P('gy', 'gx'), may hold values from -0.0390625 to 0.0390625
- attention_keep: int32 [4, 256, 6144], P('gx', None, 'gy'), may hold values 0 or 1
- feedforward_keep: int32 [4, 256, 6144], P('gx', None, 'gy'), may hold values 0 or 1
Outputs:
- block_out: bfloat16 [4, 256, 6144], P('gx', None, 'gy')
All inputs are finite; a program needn't handle non-finite values. No bound on the sum of `attention_keep` or of `feedforward_keep` on one device may be relied on, other than what follows from the above.
Results may differ from a plain program's by a relative error of at most 0.017.
Values may be sent and summed in bfloat16 or wider, within the bound.
A program may use at most 128 MiB of HBM per device.

v0:
```python
import jax
import jax.numpy as jnp
from jax import lax
from jax.sharding import PartitionSpec as P

epsilon = 1e-06
keep_scale = 1.0 / 0.9
UP_CHUNKS = 2

f32 = jnp.float32
bf16 = jnp.bfloat16


def layer_norm(values, gain):
    center = values - jnp.mean(values, axis=-1, keepdims=True)
    variance = jnp.mean(center * center, axis=-1, keepdims=True)
    return center * lax.rsqrt(variance + epsilon) * gain


def head_norm(values, gain):
    row_count = values.shape[0]
    shaped = values.reshape(row_count, -1, gain.shape[0])
    return layer_norm(shaped, gain).reshape(row_count, -1)


def mul(left, right):
    return jnp.dot(left, right, preferred_element_type=f32)


def swap(values, bit, n_gx):
    return lax.ppermute(values, "gx", [(i, i ^ bit) for i in range(n_gx)])


def scatter_sum(odd_rows, even_rows, weight, n_gx):
    received = swap(mul(odd_rows, weight).astype(bf16), 1, n_gx)
    total = mul(even_rows, weight).astype(bf16).astype(f32) + received.astype(f32)
    bit, width = 2, weight.shape[1]
    own_rows = 2 * odd_rows.shape[0] // n_gx
    while bit < n_gx:
        pairs = total.reshape(-1, 2, own_rows, width)
        received = swap(pairs[:, 1].astype(bf16), bit, n_gx)
        total = pairs[:, 0] + received.astype(f32)
        bit *= 2
    return total.reshape(own_rows, width)


def gather_pair(own, n_gx):
    held, bit = own, n_gx // 2
    while bit > 1:
        held = jnp.concatenate([held, swap(held, bit, n_gx)], axis=0)
        bit //= 2
    return held, swap(held, 1, n_gx)


def gather_order(n_gx):
    order, bit = [0], n_gx // 2
    while bit >= 1:
        order = order + [p ^ bit for p in order]
        bit //= 2
    return order


def ring_place(index, count):
    return jnp.where(index % 2 == 0, index // 2, count - 1 - index // 2)


def ring_gather(own, ring, place):
    n = len(ring)
    ahead = [(ring[r], ring[(r + 1) % n]) for r in range(n)]
    back = [(b, a) for a, b in ahead]
    forward, backward = [own], [own]
    for step in range(n // 2 - 1):
        forward.append(lax.ppermute(forward[-1], "gy", ahead))
        backward.append(lax.ppermute(backward[-1], "gy", back))
    half = own.shape[0] // 2
    far = jnp.concatenate(
        [
            lax.ppermute(forward[-1][:half], "gy", ahead),
            lax.ppermute(backward[-1][half:], "gy", back),
        ],
        axis=0,
    )
    return jnp.stack(forward + [far] + backward[:0:-1])


def ring_scatter(partial, ring, place):
    n = len(ring)
    half = partial.shape[1] // 2
    ahead = [(ring[r], ring[(r + 1) % n]) for r in range(n)]
    back = [(b, a) for a, b in ahead]

    def block(index, start):
        index = lax.rem(index + 2 * n, n)
        return lax.dynamic_slice(
            partial, (index, start, 0), (1, half, partial.shape[2])
        )[0]

    up, down = block(place - 1, 0), block(place + 1, half)
    for step in range(n - 1):
        came_up = lax.ppermute(up, "gy", ahead)
        came_down = lax.ppermute(down, "gy", back)
        up = came_up.astype(f32) + block(place - 2 - step, 0).astype(f32)
        down = came_down.astype(f32) + block(place + 2 + step, half).astype(f32)
        up, down = up.astype(bf16), down.astype(bf16)
    return jnp.concatenate([up, down], axis=0)


def per_device(
    tokens,
    norm_gain,
    qkv_weight,
    up_weight,
    query_gain,
    key_gain,
    out_weight,
    down_weight,
    attention_keep,
    feedforward_keep,
):
    n_gx, n_gy = lax.axis_size("gx"), lax.axis_size("gy")
    sub = n_gy // n_gx
    me = lax.axis_index("gx")
    ring = list(range(0, n_gy, 2)) + list(range(1, n_gy, 2))[::-1]
    place = ring_place(lax.axis_index("gy"), n_gy)
    images, seq_len, slice_width = tokens.shape
    own_rows = images * seq_len
    block_width = qkv_weight.shape[0]
    head_cols = qkv_weight.shape[2]
    head_size = query_gain.shape[0]

    flat = tokens.reshape(own_rows, slice_width)
    turned = lax.ppermute(
        flat,
        ("gx", "gy"),
        [
            (i * n_gy + k * sub + s, k * n_gy + i * sub + s)
            for i in range(n_gx)
            for k in range(n_gx)
            for s in range(sub)
        ],
    )
    gathered = ring_gather(turned, ring, place)

    wide = flat.astype(f32)
    mean = jnp.mean(wide, axis=1)
    squares = jnp.sum((wide - mean[:, None]) ** 2, axis=1)
    count, bit = slice_width, 1
    while bit < n_gy:
        pairs = [(i, i ^ bit) for i in range(n_gy)]
        other = lax.ppermute(jnp.stack([mean, squares]), "gy", pairs)
        squares = squares + other[1] + (0.5 * count) * (mean - other[0]) ** 2
        mean = 0.5 * (mean + other[0])
        count, bit = 2 * count, 2 * bit
    stats = jnp.stack([mean, lax.rsqrt(squares / count + epsilon)])[None]
    bit = 1
    while bit < n_gx:
        stats = jnp.concatenate([stats, swap(stats, bit, n_gx)], axis=0)
        bit *= 2
    gain = lax.dynamic_slice_in_dim(norm_gain, me * block_width, block_width, 0)

    def normed_rows(position):
        image = me ^ position
        rows = jnp.concatenate(
            [
                lax.dynamic_index_in_dim(
                    gathered,
                    lax.rem(place - ring_place(image * sub + s, n_gy) + n_gy, n_gy),
                    0,
                    keepdims=False,
                )
                for s in range(sub)
            ],
            axis=1,
        ).astype(f32)
        row_mean, row_scale = stats[position, 0], stats[position, 1]
        return ((rows - row_mean[:, None]) * row_scale[:, None] * gain).astype(bf16)

    odd_rows = jnp.concatenate([normed_rows(p) for p in range(1, n_gx, 2)], axis=0)
    even_rows = jnp.concatenate([normed_rows(p) for p in range(0, n_gx, 2)], axis=0)

    qkv_flat = qkv_weight.reshape(block_width, 3 * head_cols)
    united = scatter_sum(odd_rows, even_rows, qkv_flat, n_gx)
    up_cols = up_weight.shape[1] // UP_CHUNKS
    hidden = []
    for c in range(UP_CHUNKS):
        total = scatter_sum(
            odd_rows, even_rows, up_weight[:, c * up_cols : (c + 1) * up_cols], n_gx
        )
        hidden.append(jax.nn.gelu(total, approximate=False).astype(bf16))

    queries = head_norm(united[:, :head_cols], query_gain).astype(bf16)
    keys = head_norm(united[:, head_cols : 2 * head_cols], key_gain).astype(bf16)
    values = united[:, 2 * head_cols :].astype(bf16)
    query_grid = queries.reshape(images, seq_len, -1, head_size)
    key_grid = keys.reshape(images, seq_len, -1, head_size)
    value_grid = values.reshape(images, seq_len, -1, head_size)
    scores = jnp.einsum(
        "bshd,bthd->bhst", query_grid, key_grid, preferred_element_type=f32
    ) * head_size ** (-0.5)
    raised = jnp.exp(scores)
    weights = (raised / jnp.sum(raised, axis=-1, keepdims=True)).astype(bf16)
    attended = jnp.einsum("bhst,bthd->bshd", weights, value_grid, preferred_element_type=f32)
    attended = attended.astype(bf16).reshape(own_rows, head_cols)

    order = gather_order(n_gx)
    def home(devices):
        return [
            (
                k * n_gy + devices[s * n_gx + q],
                (k ^ order[q]) * n_gy + k * sub + s,
            )
            for k in range(n_gx)
            for s in range(sub)
            for q in range(n_gx)
        ]

    def columns(weight, s):
        return weight[:, s * slice_width : (s + 1) * slice_width]

    attended_halves = gather_pair(attended, n_gx)
    attention_out = lax.psum_scatter(
        jnp.concatenate(
            [
                mul(rows, columns(out_weight, s)).astype(bf16)
                for s in range(sub)
                for rows in attended_halves
            ],
            axis=0,
        ),
        "gy",
        scatter_dimension=0,
        tiled=True,
    )
    attention_out = lax.ppermute(attention_out, ("gx", "gy"), home(range(n_gy))).astype(f32)
    hidden_halves = [gather_pair(part, n_gx) for part in hidden]
    pieces = []
    for s in range(sub):
        for half in range(2):
            total = 0.0
            for c in range(UP_CHUNKS):
                weight = down_weight[c * up_cols : (c + 1) * up_cols]
                total = total + mul(hidden_halves[c][half], columns(weight, s))
            pieces.append(total.astype(bf16))
    partial = jnp.concatenate(pieces, axis=0).reshape(n_gy, own_rows, slice_width)
    feedforward_out = ring_scatter(partial, ring, place)
    feedforward_out = lax.ppermute(feedforward_out, ("gx", "gy"), home(ring)).astype(f32)

    shape = tokens.shape
    branches = attention_keep.astype(f32) * attention_out.reshape(
        shape
    ) + feedforward_keep.astype(f32) * feedforward_out.reshape(shape)
    return (tokens.astype(f32) + branches * keep_scale).astype(bf16)


def solution(mesh):
    in_specs = (
        P("gx", None, "gy"),
        P(),
        P("gx", None, "gy"),
        P("gx", "gy"),
        P(),
        P(),
        P("gy", "gx"),
        P("gy", "gx"),
        P("gx", None, "gy"),
        P("gx", None, "gy"),
    )
    out_specs = P("gx", None, "gy")
    return jax.shard_map(
        per_device, mesh=mesh, in_specs=in_specs, out_specs=out_specs, check_vma=False
    )
```

profile of v0, /device:TPU:2, one launch (start us, length us, event | category | flops | bytes accessed | tf_op | source)
XLA Modules:
  0.0 319.2 jit_solution(9035723459280658667)
XLA Ops:
  6.5 1.6 collective-permute-start
  8.2 1.1 convert_reduce_fusion
  9.3 1.2 fusion.89
  10.9 3.3 %collective-permute-done.9 = f32[2,256]{1,0:T(2,128)S(1)} collective-permute-done((f32[2,256]{1,0:T(2,128)S(1)}, f32[2,256]{1,0:T(2,128)S(1)}, u32[]{:S(2)}, u32[]{:S(2)}) %collective-permute-start.9) | collective-permute-done | bytes 2080 | tf_op jit(solution)/shard_map/ppermute | solution.py:150
  14.2 1.9 collective-permute-start.10
  16.2 1.7 collective-permute-done.10
  17.9 5.2 %collective-permute-start.11 = (f32[2,256]{1,0:T(2,128)S(1)}, f32[2,256]{1,0:T(2,128)S(1)}, u32[]{:S(2)}, u32[]{:S(2)}) collective-permute-start(f32[2,256]{1,0:T(2,128)S(1)} %pad_maximum_fusion.17), channel_id=1, source_target_pairs={{0,4},{1,5},{2,6},{3,7},{4,0},{5,1},{6,2},{7,3},{8,12},{9,13},{10,... | collective-permute-start | bytes 6152 | tf_op jit(solution)/shard_map/ppermute | solution.py:150
  23.1 6.6 %copy.13 = bf16[1536,3,512]{0,2,1:T(8,128)(2,1)} copy(bf16[1536,3,512]{2,0,1:T(8,128)(2,1)} %param.12) | data formatting | bytes 9437184 | tf_op args[2]
  31.2 1.5 collective-permute-start.5
  32.7 1.3 collective-permute-start.13
  34.1 8.1 %collective-permute-done.1 = bf16[256,768]{1,0:T(8,128)(2,1)S(1)} collective-permute-done((bf16[256,768]{1,0:T(8,128)(2,1)S(1)}, bf16[256,768]{1,0:T(8,128)(2,1)S(1)}, u32[]{:S(2)}, u32[]{:S(2)}) %collective-permute-start.1) | collective-permute-done | bytes 393248 | tf_op jit(solution)/shard_map/ppermute | solution.py:73
  42.7 1.5 collective-permute-start.6
  44.2 8.5 %collective-permute-done.2 = bf16[256,768]{1,0:T(8,128)(2,1)S(1)} collective-permute-done((bf16[256,768]{1,0:T(8,128)(2,1)S(1)}, bf16[256,768]{1,0:T(8,128)(2,1)S(1)}, u32[]{:S(2)}, u32[]{:S(2)}) %collective-permute-start.2) | collective-permute-done | bytes 393248 | tf_op jit(solution)/shard_map/ppermute | solution.py:73
  53.3 1.5 collective-permute-start.7
  54.9 7.7 %collective-permute-done.3 = bf16[256,768]{1,0:T(8,128)(2,1)S(1)} collective-permute-done((bf16[256,768]{1,0:T(8,128)(2,1)S(1)}, bf16[256,768]{1,0:T(8,128)(2,1)S(1)}, u32[]{:S(2)}, u32[]{:S(2)}) %collective-permute-start.3) | collective-permute-done | bytes 393248 | tf_op jit(solution)/shard_map/ppermute | solution.py:73
  63.1 1.7 collective-permute-start.8
  64.9 3.4 %collective-permute-done.4 = bf16[128,768]{1,0:T(8,128)(2,1)S(1)} collective-permute-done((bf16[128,768]{1,0:T(8,128)(2,1)S(1)}, bf16[128,768]{1,0:T(8,128)(2,1)S(1)}, u32[]{:S(2)}, u32[]{:S(2)}) %collective-permute-start.4) | collective-permute-done | bytes 196640 | tf_op jit(solution)/shard_map/ppermute | solution.py:78
  69.4 1.2 multiply_convert_fusion.3
  71.4 3.8 %convolution_convert_fusion = bf16[512,1536]{1,0:T(8,128)(2,1)} fusion(bf16[1536,1536]{0,1:T(8,128)(2,1)S(1)} %bitcast.325, bf16[256,1536]{1,0:T(8,128)(2,1)S(1)} %get-tuple-element.38, bf16[256,1536]{1,0:T(8,128)(2,1)S(1)} %get-tuple-element.37), kind=kOutput, calls=%fused_computation.17 | convolution fusion | flops 2419851264 | bytes 7864320 | tf_op jit(solution)/shard_map/dot_general | solution.py:27
  75.2 6.5 %fusion.17 = bf16[512,1536]{1,0:T(8,128)(2,1)} fusion(bf16[1536,3072]{1,0:T(8,128)(2,1)} %param.13, bf16[256,1536]{1,0:T(8,128)(2,1)S(1)} %get-tuple-element.38, bf16[256,1536]{1,0:T(8,128)(2,1)S(1)} %get-tuple-element.37), kind=kOutput, calls=%fused_computation.16 | convolution fusion | flops 2419851264 | bytes 7864320 | tf_op jit(solution)/shard_map/dot_general | solution.py:27
  82.3 6.4 %fusion.11 = bf16[512,1536]{1,0:T(8,128)(2,1)} fusion(bf16[1536,3072]{1,0:T(8,128)(2,1)} %param.13, bf16[256,1536]{1,0:T(8,128)(2,1)S(1)} %get-tuple-element.38, bf16[256,1536]{1,0:T(8,128)(2,1)S(1)} %get-tuple-element.37), kind=kOutput, calls=%fused_computation.14 | convolution fusion | flops 2419851264 | bytes 7864320 | tf_op jit(solution)/shard_map/dot_general | solution.py:27
  88.8 4.0 %convert_add_fusion.2 = f32[512,1536]{1,0:T(8,128)S(1)} fusion(bf16[512,1536]{1,0:T(8,128)(2,1)} %collective-permute-done.14, bf16[1536,1536]{0,1:T(8,128)(2,1)S(1)} %bitcast.328, bf16[256,1536]{1,0:T(8,128)(2,1)S(1)} %get-tuple-element.36, bf16[256,1536]{1,0:T(8,128)(2,1)S(1)} %get-tuple-element.35), kind=kOutput, calls=%fused_computation.12 | convolution fusion | flops 2422210560 | bytes 11010048 | tf_op jit(solution)/shard_map/dot_general | solution.py:27
  94.5 2.4 copy.23
  96.9 5.4 %convert_add_fusion = f32[512,1536]{1,0:T(8,128)S(1)} fusion(bf16[512,1536]{1,0:T(8,128)(2,1)} %collective-permute-done.22, bf16[1536,3072]{1,0:T(8,128)(2,1)} %param.13, bf16[256,1536]{1,0:T(8,128)(2,1)S(1)} %copy-done.8, bf16[256,1536]{1,0:T(8,128)(2,1)S(1)} %copy-done.6), kind=kOutput, calls=%fused_computation.10 | convolution fusion | flops 2422210560 | bytes 11010048 | tf_op jit(solution)/shard_map/dot_general | solution.py:27
  103.4 2.0 collective-permute-start.23
  105.5 5.4 %convert_add_fusion.1 = f32[512,1536]{1,0:T(8,128)S(1)} fusion(bf16[512,1536]{1,0:T(8,128)(2,1)} %collective-permute-done.19, bf16[1536,3072]{1,0:T(8,128)(2,1)} %param.13, bf16[256,1536]{1,0:T(8,128)(2,1)S(1)} %copy-done.8, bf16[256,1536]{1,0:T(8,128)(2,1)S(1)} %copy-done.6), kind=kOutput, calls=%fused_computation.11 | convolution fusion | flops 2422210560 | bytes 11010048 | tf_op jit(solution)/shard_map/dot_general | solution.py:27
  111.3 6.2 %collective-permute-done.15 = bf16[1,256,1536]{1,2,0:T(8,128)(2,1)S(1)} collective-permute-done((bf16[1,256,1536]{1,2,0:T(8,128)(2,1)}, bf16[1,256,1536]{1,2,0:T(8,128)(2,1)S(1)}, u32[]{:S(2)}, u32[]{:S(2)}) %collective-permute-start.15) | collective-permute-done | bytes 786464 | tf_op jit(solution)/shard_map/ppermute | solution.py:31
  119.0 15.5 %collective-permute-done.23 = bf16[1,256,1536]{2,1,0:T(8,128)(2,1)} collective-permute-done((bf16[1,256,1536]{2,1,0:T(8,128)(2,1)}, bf16[1,256,1536]{2,1,0:T(8,128)(2,1)}, u32[]{:S(2)}, u32[]{:S(2)}) %collective-permute-start.23) | collective-permute-done | bytes 786464 | tf_op jit(solution)/shard_map/ppermute | solution.py:31
  134.5 4.8 %fusion.45 = bf16[256,1536]{1,0:T(8,128)(2,1)S(1)} fusion(bf16[1,256,1536]{2,1,0:T(8,128)(2,1)} %collective-permute-done.23, f32[1,2,256,1536]{3,2,1,0:T(8,128)} %bitcast.331), kind=kLoop, calls=%fused_computation.42 | loop fusion | flops 26345472 | bytes 3145728 | tf_op jit(solution)/shard_map/convert_element_type | solution.py:189
  139.4 12.0 %collective-permute-done.20 = bf16[1,256,1536]{2,1,0:T(8,128)(2,1)} collective-permute-done((bf16[1,256,1536]{2,1,0:T(8,128)(2,1)S(1)}, bf16[1,256,1536]{2,1,0:T(8,128)(2,1)}, u32[]{:S(2)}, u32[]{:S(2)}) %collective-permute-start.20) | collective-permute-done | bytes 786464 | tf_op jit(solution)/shard_map/ppermute | solution.py:31
  151.4 4.5 %fusion.42 = bf16[256,1536]{1,0:T(8,128)(2,1)S(1)} fusion(bf16[1,256,1536]{2,1,0:T(8,128)(2,1)} %collective-permute-done.20, f32[1,2,256,1536]{3,2,1,0:T(8,128)S(1)} %bitcast.333), kind=kLoop, calls=%fused_computation.39 | loop fusion | flops 26345472 | bytes 3145728 | tf_op jit(solution)/shard_map/convert_element_type | solution.py:189
  160.1 1.8 pad_maximum_fusion
  162.0 28.1 %collective-permute-done.21 = bf16[256,1536]{1,0:T(8,128)(2,1)S(1)} collective-permute-done((bf16[256,1536]{1,0:T(8,128)(2,1)S(1)}, bf16[256,1536]{1,0:T(8,128)(2,1)S(1)}, u32[]{:S(2)}, u32[]{:S(2)}) %collective-permute-start.21) | collective-permute-done | bytes 786464 | tf_op jit(solution)/shard_map/ppermute | solution.py:31
  190.9 3.2 %fusion.34 = f32[512,768]{1,0:T(8,128)S(1)} fusion(bf16[3072,1536]{1,0:T(8,128)(2,1)} %param.17, bf16[256,1536]{1,0:T(8,128)(2,1)S(1)} %collective-permute-done.24, bf16[256,1536]{1,0:T(8,128)(2,1)S(1)} %fusion.45), kind=kOutput, calls=%fused_computation.31 | convolution fusion | flops 1211105280 | bytes 5505024 | tf_op jit(solution)/shard_map/dot_general | solution.py:27
  194.2 3.2 add_convert_fusion.3
  197.4 1.4 fusion.26
  198.8 1.4 add_convert_fusion.1
  200.2 1.4 fusion.32
  201.6 1.4 fusion.24
  203.0 1.4 add_convert_fusion.2
  204.4 1.4 add_convert_fusion
  207.1 1.2 collective-permute-start.34
  208.3 4.9 %collective-permute-done.27 = bf16[128,768]{1,0:T(8,128)(2,1)} collective-permute-done((bf16[128,768]{1,0:T(8,128)(2,1)S(1)}, bf16[128,768]{1,0:T(8,128)(2,1)}, u32[]{:S(2)}, u32[]{:S(2)}) %collective-permute-start.27) | collective-permute-done | bytes 196640 | tf_op jit(solution)/shard_map/ppermute | solution.py:100
  214.1 1.3 fusion.123
  215.9 1.6 collective-permute-start.35
  217.5 4.0 %collective-permute-done.28 = bf16[128,768]{1,0:T(8,128)(2,1)S(1)} collective-permute-done((bf16[128,768]{1,0:T(8,128)(2,1)S(1)}, bf16[128,768]{1,0:T(8,128)(2,1)S(1)}, u32[]{:S(2)}, u32[]{:S(2)}) %collective-permute-start.28) | collective-permute-done | bytes 196640 | tf_op jit(solution)/shard_map/ppermute | solution.py:100
  221.5 3.2 collective-permute-done.35
  225.9 2.0 collective-permute-start.36
  227.9 9.0 %collective-permute-done.29 = bf16[128,768]{1,0:T(8,128)(2,1)S(1)} collective-permute-done((bf16[128,768]{1,0:T(8,128)(2,1)S(1)}, bf16[128,768]{1,0:T(8,128)(2,1)S(1)}, u32[]{:S(2)}, u32[]{:S(2)}) %collective-permute-start.29) | collective-permute-done | bytes 196640 | tf_op jit(solution)/shard_map/ppermute | solution.py:100
  238.0 1.9 collective-permute-start.30
  240.1 3.6 %collective-permute-done.30 = bf16[128,768]{1,0:T(8,128)(2,1)S(1)} collective-permute-done((bf16[128,768]{1,0:T(8,128)(2,1)S(1)}, bf16[128,768]{1,0:T(8,128)(2,1)S(1)}, u32[]{:S(2)}, u32[]{:S(2)}) %collective-permute-start.30) | collective-permute-done | bytes 196640 | tf_op jit(solution)/shard_map/ppermute | solution.py:100
  243.7 1.9 collective-permute-done.37
  246.7 1.7 collective-permute-start.31
  248.8 3.9 %collective-permute-done.31 = bf16[128,768]{1,0:T(8,128)(2,1)S(1)} collective-permute-done((bf16[128,768]{1,0:T(8,128)(2,1)S(1)}, bf16[128,768]{1,0:T(8,128)(2,1)S(1)}, u32[]{:S(2)}, u32[]{:S(2)}) %collective-permute-start.31) | collective-permute-done | bytes 196640 | tf_op jit(solution)/shard_map/ppermute | solution.py:100
  252.7 1.8 collective-permute-done.38
  255.8 1.9 collective-permute-start.39
  257.7 5.2 %collective-permute-done.32 = bf16[128,768]{1,0:T(8,128)(2,1)S(1)} collective-permute-done((bf16[128,768]{1,0:T(8,128)(2,1)S(1)}, bf16[128,768]{1,0:T(8,128)(2,1)S(1)}, u32[]{:S(2)}, u32[]{:S(2)}) %collective-permute-start.32) | collective-permute-done | bytes 196640 | tf_op jit(solution)/shard_map/ppermute | solution.py:100
  264.1 2.7 collective-permute-start.33
  266.9 3.3 %collective-permute-done.33 = bf16[128,768]{1,0:T(8,128)(2,1)S(1)} collective-permute-done((bf16[128,768]{1,0:T(8,128)(2,1)S(1)}, bf16[128,768]{1,0:T(8,128)(2,1)S(1)}, u32[]{:S(2)}, u32[]{:S(2)}) %collective-permute-start.33) | collective-permute-done | bytes 196640 | tf_op jit(solution)/shard_map/ppermute | solution.py:100
  270.1 2.4 collective-permute-done.40
  273.7 1.9 collective-permute-start.41
  275.6 2.5 collective-permute-start.18
  278.1 10.9 %collective-permute-done.41 = bf16[256,768]{1,0:T(8,128)(2,1)S(1)} collective-permute-done((bf16[256,768]{1,0:T(8,128)(2,1)S(1)}, bf16[256,768]{1,0:T(8,128)(2,1)S(1)}, u32[]{:S(2)}, u32[]{:S(2)}) %collective-permute-start.41) | collective-permute-done | bytes 393248 | tf_op jit(solution)/shard_map/ppermute | solution.py:246
  289.0 22.3 %collective-permute-done.18 = bf16[256,768]{1,0:T(8,128)(2,1)S(1)} collective-permute-done((bf16[256,768]{1,0:T(8,128)(2,1)}, bf16[256,768]{1,0:T(8,128)(2,1)S(1)}, u32[]{:S(2)}, u32[]{:S(2)}) %collective-permute-start.18) | collective-permute-done | bytes 393248 | tf_op jit(solution)/shard_map/ppermute | solution.py:234
  (148 shorter events, 26.7 us)
Async XLA Ops:
  6.5 269.1 %reduce-scatter.2.cloned.1.call-start = ((), (), s32[]{:S(2)}) async-start(), calls=%async_computation.1 | async-start | bytes 3538944 | tf_op jit(solution)/shard_map/reduce_scatter | solution.py:221
  6.5 24.1 %collective-permute-start = (bf16[256,768]{1,0:T(8,128)(2,1)}, bf16[256,768]{1,0:T(8,128)(2,1)S(1)}, u32[]{:S(2)}, u32[]{:S(2)}) collective-permute-start(bf16[256,768]{1,0:T(8,128)(2,1)} %bitcast.329), channel_id=1, source_target_pairs={{0,0},{1,1},{2,8},{3,9},{4,16},{5,17},{6,24},{7,25},{8,2},{9,3},{1... | collective-permute-start | bytes 1179656 | tf_op jit(solution)/shard_map/ppermute | solution.py:132
  10.6 3.7 %collective-permute-start.9 = (f32[2,256]{1,0:T(2,128)S(1)}, f32[2,256]{1,0:T(2,128)S(1)}, u32[]{:S(2)}, u32[]{:S(2)}) collective-permute-start(f32[2,256]{1,0:T(2,128)S(1)} %pad_maximum_fusion.15), channel_id=1, source_target_pairs={{0,1},{1,0},{2,3},{3,2},{4,5},{5,4},{6,7},{7,6},{8,9},{9,8},{10,11... | collective-permute-start | bytes 6152 | tf_op jit(solution)/shard_map/ppermute | solution.py:150
  14.2 3.7 %collective-permute-start.10 = (f32[2,256]{1,0:T(2,128)S(1)}, f32[2,256]{1,0:T(2,128)S(1)}, u32[]{:S(2)}, u32[]{:S(2)}) collective-permute-start(f32[2,256]{1,0:T(2,128)S(1)} %pad_maximum_fusion.16), channel_id=1, source_target_pairs={{0,2},{1,3},{2,0},{3,1},{4,6},{5,7},{6,4},{7,5},{8,10},{9,11},{10,... | collective-permute-start | bytes 6152 | tf_op jit(solution)/shard_map/ppermute | solution.py:150
  17.9 12.6 %collective-permute-start.11 = (f32[2,256]{1,0:T(2,128)S(1)}, f32[2,256]{1,0:T(2,128)S(1)}, u32[]{:S(2)}, u32[]{:S(2)}) collective-permute-start(f32[2,256]{1,0:T(2,128)S(1)} %pad_maximum_fusion.17), channel_id=1, source_target_pairs={{0,4},{1,5},{2,6},{3,7},{4,0},{5,1},{6,2},{7,3},{8,12},{9,13},{10,... | collective-permute-start | bytes 6152 | tf_op jit(solution)/shard_map/ppermute | solution.py:150
  30.6 2.2 collective-permute-start.12
  30.6 11.5 %collective-permute-start.1 = (bf16[256,768]{1,0:T(8,128)(2,1)S(1)}, bf16[256,768]{1,0:T(8,128)(2,1)S(1)}, u32[]{:S(2)}, u32[]{:S(2)}) collective-permute-start(bf16[256,768]{1,0:T(8,128)(2,1)S(1)} %collective-permute-done), channel_id=1, source_target_pairs={{0,2},{2,4},{4,6},{6,7},{7,5},{5,3},{3,1},{1,0},{8,10},{10,12},{12... | collective-permute-start | bytes 1179656 | tf_op jit(solution)/shard_map/ppermute | solution.py:73
  31.2 11.5 %collective-permute-start.5 = (bf16[256,768]{1,0:T(8,128)(2,1)S(1)}, bf16[256,768]{1,0:T(8,128)(2,1)S(1)}, u32[]{:S(2)}, u32[]{:S(2)}) collective-permute-start(bf16[256,768]{1,0:T(8,128)(2,1)S(1)} %collective-permute-done), channel_id=1, source_target_pairs={{2,0},{4,2},{6,4},{7,6},{5,7},{3,5},{1,3},{0,1},{10,8},{12,10},{14... | collective-permute-start | bytes 1179656 | tf_op jit(solution)/shard_map/ppermute | solution.py:74
  32.7 11.5 %collective-permute-start.13 = (f32[2,2,256]{2,1,0:T(2,128)S(1)}, f32[2,2,256]{2,1,0:T(2,128)S(1)}, u32[]{:S(2)}, u32[]{:S(2)}) collective-permute-start(f32[2,2,256]{2,1,0:T(2,128)S(1)} %pad_maximum_fusion.14), channel_id=1, source_target_pairs={{0,16},{8,24},{16,0},{24,8},{1,17},{9,25},{17,1},{25,9},{2,18},{10... | collective-permute-start | bytes 12296 | tf_op jit(solution)/shard_map/ppermute | solution.py:31
  42.2 10.6 %collective-permute-start.2 = (bf16[256,768]{1,0:T(8,128)(2,1)S(1)}, bf16[256,768]{1,0:T(8,128)(2,1)S(1)}, u32[]{:S(2)}, u32[]{:S(2)}) collective-permute-start(bf16[256,768]{1,0:T(8,128)(2,1)S(1)} %collective-permute-done.1), channel_id=1, source_target_pairs={{0,2},{2,4},{4,6},{6,7},{7,5},{5,3},{3,1},{1,0},{8,10},{10,12},{12... | collective-permute-start | bytes 1179656 | tf_op jit(solution)/shard_map/ppermute | solution.py:73
  42.7 10.6 %collective-permute-start.6 = (bf16[256,768]{1,0:T(8,128)(2,1)S(1)}, bf16[256,768]{1,0:T(8,128)(2,1)S(1)}, u32[]{:S(2)}, u32[]{:S(2)}) collective-permute-start(bf16[256,768]{1,0:T(8,128)(2,1)S(1)} %collective-permute-done.5), channel_id=1, source_target_pairs={{2,0},{4,2},{6,4},{7,6},{5,7},{3,5},{1,3},{0,1},{10,8},{12,10},{14... | collective-permute-start | bytes 1179656 | tf_op jit(solution)/shard_map/ppermute | solution.py:74
  52.8 9.7 %collective-permute-start.3 = (bf16[256,768]{1,0:T(8,128)(2,1)S(1)}, bf16[256,768]{1,0:T(8,128)(2,1)S(1)}, u32[]{:S(2)}, u32[]{:S(2)}) collective-permute-start(bf16[256,768]{1,0:T(8,128)(2,1)S(1)} %collective-permute-done.2), channel_id=1, source_target_pairs={{0,2},{2,4},{4,6},{6,7},{7,5},{5,3},{3,1},{1,0},{8,10},{10,12},{12... | collective-permute-start | bytes 1179656 | tf_op jit(solution)/shard_map/ppermute | solution.py:73
  53.3 9.8 %collective-permute-start.7 = (bf16[256,768]{1,0:T(8,128)(2,1)S(1)}, bf16[256,768]{1,0:T(8,128)(2,1)S(1)}, u32[]{:S(2)}, u32[]{:S(2)}) collective-permute-start(bf16[256,768]{1,0:T(8,128)(2,1)S(1)} %collective-permute-done.6), channel_id=1, source_target_pairs={{2,0},{4,2},{6,4},{7,6},{5,7},{3,5},{1,3},{0,1},{10,8},{12,10},{14... | collective-permute-start | bytes 1179656 | tf_op jit(solution)/shard_map/ppermute | solution.py:74
  62.5 5.7 %collective-permute-start.4 = (bf16[128,768]{1,0:T(8,128)(2,1)S(1)}, bf16[128,768]{1,0:T(8,128)(2,1)S(1)}, u32[]{:S(2)}, u32[]{:S(2)}) collective-permute-start(bf16[128,768]{1,0:T(8,128)(2,1)S(1)} %slice.157), channel_id=1, source_target_pairs={{0,2},{2,4},{4,6},{6,7},{7,5},{5,3},{3,1},{1,0},{8,10},{10,12},{12... | collective-permute-start | bytes 589832 | tf_op jit(solution)/shard_map/ppermute | solution.py:78
  63.1 5.9 %collective-permute-start.8 = (bf16[128,768]{1,0:T(8,128)(2,1)S(1)}, bf16[128,768]{1,0:T(8,128)(2,1)S(1)}, u32[]{:S(2)}, u32[]{:S(2)}) collective-permute-start(bf16[128,768]{1,0:T(8,128)(2,1)S(1)} %slice.158), channel_id=1, source_target_pairs={{2,0},{4,2},{6,4},{7,6},{5,7},{3,5},{1,3},{0,1},{10,8},{12,10},{14... | collective-permute-start | bytes 589832 | tf_op jit(solution)/shard_map/ppermute | solution.py:79
  69.1 2.2 slice-start
  69.2 2.3 slice-start.1
  70.6 18.1 %copy-start.5 = (bf16[256,1536]{1,0:T(8,128)(2,1)}, bf16[256,1536]{1,0:T(8,128)(2,1)S(1)}, u32[]{:S(2)}) copy-start(bf16[256,1536]{1,0:T(8,128)(2,1)S(1)} %get-tuple-element.35) | copy-start | bytes 2359300
  70.7 18.1 %copy-start.7 = (bf16[256,1536]{1,0:T(8,128)(2,1)}, bf16[256,1536]{1,0:T(8,128)(2,1)S(1)}, u32[]{:S(2)}) copy-start(bf16[256,1536]{1,0:T(8,128)(2,1)S(1)} %get-tuple-element.36) | copy-start | bytes 2359300
  75.2 13.6 %collective-permute-start.14 = (bf16[512,1536]{1,0:T(8,128)(2,1)}, bf16[512,1536]{1,0:T(8,128)(2,1)}, u32[]{:S(2)}, u32[]{:S(2)}) collective-permute-start(bf16[512,1536]{1,0:T(8,128)(2,1)} %convolution_convert_fusion), channel_id=1, source_target_pairs={{0,8},{8,0},{16,24},{24,16},{1,9},{9,1},{17,25},{25,17},{2,10},{10... | collective-permute-start | bytes 4718600 | tf_op jit(solution)/shard_map/ppermute | solution.py:31
  75.2 7.0 %copy-start.11 = (f32[128]{0:T(128)S(1)}, f32[128]{0:T(128)}, u32[]{:S(2)}) copy-start(f32[128]{0:T(128)} %param.15) | copy-start | bytes 1540
  75.2 7.0 %copy-start.12 = (f32[128]{0:T(128)S(1)}, f32[128]{0:T(128)}, u32[]{:S(2)}) copy-start(f32[128]{0:T(128)} %param.14) | copy-start | bytes 1540
  75.2 13.6 %slice-start.2 = ((s8[4718592]{0:T(1024)(128)(4,1)}), s8[4194304]{0:T(1024)(128)(4,1)S(1)}, s32[]{:S(2)}) async-start(s8[4718592]{0:T(1024)(128)(4,1)} %bitcast.326), calls=%async_computation.4 | async-start | bytes 8388608
  81.8 7.0 %slice-start.3 = ((s8[4718592]{0:T(1024)(128)(4,1)}), s8[524288]{0:T(1024)(128)(4,1)S(1)}, s32[]{:S(2)}) async-start(s8[4718592]{0:T(1024)(128)(4,1)} %bitcast.326), calls=%async_computation.5 | async-start | bytes 1048576
  81.8 15.1 %collective-permute-start.22 = (bf16[512,1536]{1,0:T(8,128)(2,1)}, bf16[512,1536]{1,0:T(8,128)(2,1)}, u32[]{:S(2)}, u32[]{:S(2)}) collective-permute-start(bf16[512,1536]{1,0:T(8,128)(2,1)} %fusion.17), channel_id=1, source_target_pairs={{0,8},{8,0},{16,24},{24,16},{1,9},{9,1},{17,25},{25,17},{2,10},{10... | collective-permute-start | bytes 4718600 | tf_op jit(solution)/shard_map/ppermute | solution.py:31
  88.7 16.7 %collective-permute-start.19 = (bf16[512,1536]{1,0:T(8,128)(2,1)}, bf16[512,1536]{1,0:T(8,128)(2,1)}, u32[]{:S(2)}, u32[]{:S(2)}) collective-permute-start(bf16[512,1536]{1,0:T(8,128)(2,1)} %fusion.11), channel_id=1, source_target_pairs={{0,8},{8,0},{16,24},{24,16},{1,9},{9,1},{17,25},{25,17},{2,10},{10... | collective-permute-start | bytes 4718600 | tf_op jit(solution)/shard_map/ppermute | solution.py:31
  94.5 2.5 copy-start.6
  94.5 2.5 copy-start.8
  96.9 20.6 %collective-permute-start.15 = (bf16[1,256,1536]{1,2,0:T(8,128)(2,1)}, bf16[1,256,1536]{1,2,0:T(8,128)(2,1)S(1)}, u32[]{:S(2)}, u32[]{:S(2)}) collective-permute-start(bf16[1,256,1536]{1,2,0:T(8,128)(2,1)} %bitcast.338), channel_id=1, source_target_pairs={{0,16},{8,24},{16,0},{24,8},{1,17},{9,25},{17,1},{25,9},{2,18},{10... | collective-permute-start | bytes 2359304 | tf_op jit(solution)/shard_map/ppermute | solution.py:31
  102.4 8.5 %copy-start.2 = (f32[512,1536]{1,0:T(8,128)}, f32[512,1536]{1,0:T(8,128)S(1)}, u32[]{:S(2)}) copy-start(f32[512,1536]{1,0:T(8,128)S(1)} %convert_add_fusion) | copy-start | bytes 9437188
  103.4 31.1 %collective-permute-start.23 = (bf16[1,256,1536]{2,1,0:T(8,128)(2,1)}, bf16[1,256,1536]{2,1,0:T(8,128)(2,1)}, u32[]{:S(2)}, u32[]{:S(2)}) collective-permute-start(bf16[1,256,1536]{2,1,0:T(8,128)(2,1)} %fusion.91), channel_id=1, source_target_pairs={{0,16},{8,24},{16,0},{24,8},{1,17},{9,25},{17,1},{25,9},{2,18},{10... | collective-permute-start | bytes 2359304 | tf_op jit(solution)/shard_map/ppermute | solution.py:31
  110.9 6.8 %copy-start.3 = (f32[512,1536]{1,0:T(8,128)}, f32[512,1536]{1,0:T(8,128)S(1)}, u32[]{:S(2)}) copy-start(f32[512,1536]{1,0:T(8,128)S(1)} %convert_add_fusion.1) | copy-start | bytes 9437188
  111.0 40.4 %collective-permute-start.20 = (bf16[1,256,1536]{2,1,0:T(8,128)(2,1)S(1)}, bf16[1,256,1536]{2,1,0:T(8,128)(2,1)}, u32[]{:S(2)}, u32[]{:S(2)}) collective-permute-start(bf16[1,256,1536]{2,1,0:T(8,128)(2,1)S(1)} %fusion.90), channel_id=1, source_target_pairs={{0,16},{8,24},{16,0},{24,8},{1,17},{9,25},{17,1},{25,9},{2,18},{10... | collective-permute-start | bytes 2359304 | tf_op jit(solution)/shard_map/ppermute | solution.py:31
  118.9 32.4 %copy-start.4 = (f32[512,1536]{1,0:T(8,128)S(1)}, f32[512,1536]{1,0:T(8,128)}, u32[]{:S(2)}) copy-start(f32[512,1536]{1,0:T(8,128)} %copy-done.3) | copy-start | bytes 9437188
  119.0 37.9 %collective-permute-start.16 = (bf16[256,512]{0,1:T(8,128)(2,1)S(1)}, bf16[256,512]{0,1:T(8,128)(2,1)S(1)}, u32[]{:S(2)}, u32[]{:S(2)}) collective-permute-start(bf16[256,512]{0,1:T(8,128)(2,1)S(1)} %bitcast.340), channel_id=1, source_target_pairs={{0,16},{8,24},{16,0},{24,8},{1,17},{9,25},{17,1},{25,9},{2,18},{10... | collective-permute-start | bytes 786440 | tf_op jit(solution)/shard_map/ppermute | solution.py:31
  139.3 17.7 %copy-start.13 = (bf16[512,1536]{1,0:T(8,128)(2,1)S(1)}, bf16[512,1536]{1,0:T(8,128)(2,1)}, u32[]{:S(2)}) copy-start(bf16[512,1536]{1,0:T(8,128)(2,1)} %param.16) | copy-start | bytes 4718596
  139.3 51.0 %collective-permute-start.24 = (bf16[256,1536]{1,0:T(8,128)(2,1)S(1)}, bf16[256,1536]{1,0:T(8,128)(2,1)S(1)}, u32[]{:S(2)}, u32[]{:S(2)}) collective-permute-start(bf16[256,1536]{1,0:T(8,128)(2,1)S(1)} %fusion.45), channel_id=1, source_target_pairs={{0,16},{8,24},{16,0},{24,8},{1,17},{9,25},{17,1},{25,9},{2,18},{10... | collective-permute-start | bytes 2359304 | tf_op jit(solution)/shard_map/ppermute | solution.py:31
  155.9 34.2 %collective-permute-start.21 = (bf16[256,1536]{1,0:T(8,128)(2,1)S(1)}, bf16[256,1536]{1,0:T(8,128)(2,1)S(1)}, u32[]{:S(2)}, u32[]{:S(2)}) collective-permute-start(bf16[256,1536]{1,0:T(8,128)(2,1)S(1)} %fusion.42), channel_id=1, source_target_pairs={{0,16},{8,24},{16,0},{24,8},{1,17},{9,25},{17,1},{25,9},{2,18},{10... | collective-permute-start | bytes 2359304 | tf_op jit(solution)/shard_map/ppermute | solution.py:31
  156.9 2.0 collective-permute-start.17
  190.1 12.8 %collective-permute-start.25 = (bf16[512,1536]{1,0:T(8,128)(2,1)S(1)}, bf16[512,1536]{1,0:T(8,128)(2,1)S(1)}, u32[]{:S(2)}, u32[]{:S(2)}) collective-permute-start(bf16[512,1536]{1,0:T(8,128)(2,1)S(1)} %pad_maximum_fusion.4), channel_id=1, source_target_pairs={{0,8},{8,0},{16,24},{24,16},{1,9},{9,1},{17,25},{25,17},{2,10},{10... | collective-permute-start | bytes 4718600 | tf_op jit(solution)/shard_map/ppermute | solution.py:31
  190.4 9.9 %collective-permute-start.26 = (bf16[512,1536]{1,0:T(8,128)(2,1)S(1)}, bf16[512,1536]{1,0:T(8,128)(2,1)S(1)}, u32[]{:S(2)}, u32[]{:S(2)}) collective-permute-start(bf16[512,1536]{1,0:T(8,128)(2,1)S(1)} %pad_maximum_fusion.5), channel_id=1, source_target_pairs={{0,8},{8,0},{16,24},{24,16},{1,9},{9,1},{17,25},{25,17},{2,10},{10... | collective-permute-start | bytes 4718600 | tf_op jit(solution)/shard_map/ppermute | solution.py:31
  190.9 6.4 %slice-start.4 = ((s8[9437184]{0:T(1024)(128)(4,1)}), s8[4194304]{0:T(1024)(128)(4,1)S(1)}, s32[]{:S(2)}) async-start(s8[9437184]{0:T(1024)(128)(4,1)} %bitcast.356), calls=%async_computation.6 | async-start | bytes 8388608
  190.9 6.4 %slice-start.5 = ((s8[9437184]{0:T(1024)(128)(4,1)}), s8[4194304]{0:T(1024)(128)(4,1)S(1)}, s32[]{:S(2)}) async-start(s8[9437184]{0:T(1024)(128)(4,1)} %bitcast.356), calls=%async_computation.7 | async-start | bytes 8388608
  194.1 3.2 %slice-start.6 = ((s8[9437184]{0:T(1024)(128)(4,1)}), s8[1048576]{0:T(1024)(128)(4,1)S(1)}, s32[]{:S(2)}) async-start(s8[9437184]{0:T(1024)(128)(4,1)} %bitcast.356), calls=%async_computation.8 | async-start | bytes 2097152
  206.2 7.9 %copy-start = (bf16[2048,768]{1,0:T(8,128)(2,1)}, bf16[2048,768]{1,0:T(8,128)(2,1)S(1)}, u32[]{:S(2)}) copy-start(bf16[2048,768]{1,0:T(8,128)(2,1)S(1)} %pad_maximum_fusion.1) | copy-start | bytes 9437188
  206.2 7.0 %collective-permute-start.27 = (bf16[128,768]{1,0:T(8,128)(2,1)S(1)}, bf16[128,768]{1,0:T(8,128)(2,1)}, u32[]{:S(2)}, u32[]{:S(2)}) collective-permute-start(bf16[128,768]{1,0:T(8,128)(2,1)S(1)} %get-tuple-element.23), channel_id=1, source_target_pairs={{0,2},{2,4},{4,6},{6,7},{7,5},{5,3},{3,1},{1,0},{8,10},{10,12},{12... | collective-permute-start | bytes 589832 | tf_op jit(solution)/shard_map/ppermute | solution.py:100
  207.1 7.0 %collective-permute-start.34 = (bf16[128,768]{1,0:T(8,128)(2,1)S(1)}, bf16[128,768]{1,0:T(8,128)(2,1)}, u32[]{:S(2)}, u32[]{:S(2)}) collective-permute-start(bf16[128,768]{1,0:T(8,128)(2,1)S(1)} %get-tuple-element.24), channel_id=1, source_target_pairs={{2,0},{4,2},{6,4},{7,6},{5,7},{3,5},{1,3},{0,1},{10,8},{12,10},{14... | collective-permute-start | bytes 589832 | tf_op jit(solution)/shard_map/ppermute | solution.py:101
  215.4 6.1 %collective-permute-start.28 = (bf16[128,768]{1,0:T(8,128)(2,1)S(1)}, bf16[128,768]{1,0:T(8,128)(2,1)S(1)}, u32[]{:S(2)}, u32[]{:S(2)}) collective-permute-start(bf16[128,768]{1,0:T(8,128)(2,1)S(1)} %get-tuple-element.21), channel_id=1, source_target_pairs={{0,2},{2,4},{4,6},{6,7},{7,5},{5,3},{3,1},{1,0},{8,10},{10,12},{12... | collective-permute-start | bytes 589832 | tf_op jit(solution)/shard_map/ppermute | solution.py:100
  215.9 8.8 %collective-permute-start.35 = (bf16[128,768]{1,0:T(8,128)(2,1)S(1)}, bf16[128,768]{1,0:T(8,128)(2,1)S(1)}, u32[]{:S(2)}, u32[]{:S(2)}) collective-permute-start(bf16[128,768]{1,0:T(8,128)(2,1)S(1)} %get-tuple-element.22), channel_id=1, source_target_pairs={{2,0},{4,2},{6,4},{7,6},{5,7},{3,5},{1,3},{0,1},{10,8},{12,10},{14... | collective-permute-start | bytes 589832 | tf_op jit(solution)/shard_map/ppermute | solution.py:101
  225.8 11.1 %collective-permute-start.29 = (bf16[128,768]{1,0:T(8,128)(2,1)S(1)}, bf16[128,768]{1,0:T(8,128)(2,1)S(1)}, u32[]{:S(2)}, u32[]{:S(2)}) collective-permute-start(bf16[128,768]{1,0:T(8,128)(2,1)S(1)} %get-tuple-element.19), channel_id=1, source_target_pairs={{0,2},{2,4},{4,6},{6,7},{7,5},{5,3},{3,1},{1,0},{8,10},{10,12},{12... | collective-permute-start | bytes 589832 | tf_op jit(solution)/shard_map/ppermute | solution.py:100
  225.9 11.0 %collective-permute-start.36 = (bf16[128,768]{1,0:T(8,128)(2,1)S(1)}, bf16[128,768]{1,0:T(8,128)(2,1)S(1)}, u32[]{:S(2)}, u32[]{:S(2)}) collective-permute-start(bf16[128,768]{1,0:T(8,128)(2,1)S(1)} %get-tuple-element.20), channel_id=1, source_target_pairs={{2,0},{4,2},{6,4},{7,6},{5,7},{3,5},{1,3},{0,1},{10,8},{12,10},{14... | collective-permute-start | bytes 589832 | tf_op jit(solution)/shard_map/ppermute | solution.py:101
  238.0 5.7 %collective-permute-start.30 = (bf16[128,768]{1,0:T(8,128)(2,1)S(1)}, bf16[128,768]{1,0:T(8,128)(2,1)S(1)}, u32[]{:S(2)}, u32[]{:S(2)}) collective-permute-start(bf16[128,768]{1,0:T(8,128)(2,1)S(1)} %get-tuple-element.17), channel_id=1, source_target_pairs={{0,2},{2,4},{4,6},{6,7},{7,5},{5,3},{3,1},{1,0},{8,10},{10,12},{12... | collective-permute-start | bytes 589832 | tf_op jit(solution)/shard_map/ppermute | solution.py:100
  239.9 5.7 %collective-permute-start.37 = (bf16[128,768]{1,0:T(8,128)(2,1)S(1)}, bf16[128,768]{1,0:T(8,128)(2,1)S(1)}, u32[]{:S(2)}, u32[]{:S(2)}) collective-permute-start(bf16[128,768]{1,0:T(8,128)(2,1)S(1)} %get-tuple-element.18), channel_id=1, source_target_pairs={{2,0},{4,2},{6,4},{7,6},{5,7},{3,5},{1,3},{0,1},{10,8},{12,10},{14... | collective-permute-start | bytes 589832 | tf_op jit(solution)/shard_map/ppermute | solution.py:101
  246.7 6.0 %collective-permute-start.31 = (bf16[128,768]{1,0:T(8,128)(2,1)S(1)}, bf16[128,768]{1,0:T(8,128)(2,1)S(1)}, u32[]{:S(2)}, u32[]{:S(2)}) collective-permute-start(bf16[128,768]{1,0:T(8,128)(2,1)S(1)} %get-tuple-element.15), channel_id=1, source_target_pairs={{0,2},{2,4},{4,6},{6,7},{7,5},{5,3},{3,1},{1,0},{8,10},{10,12},{12... | collective-permute-start | bytes 589832 | tf_op jit(solution)/shard_map/ppermute | solution.py:100
  248.4 6.1 %collective-permute-start.38 = (bf16[128,768]{1,0:T(8,128)(2,1)S(1)}, bf16[128,768]{1,0:T(8,128)(2,1)S(1)}, u32[]{:S(2)}, u32[]{:S(2)}) collective-permute-start(bf16[128,768]{1,0:T(8,128)(2,1)S(1)} %get-tuple-element.16), channel_id=1, source_target_pairs={{2,0},{4,2},{6,4},{7,6},{5,7},{3,5},{1,3},{0,1},{10,8},{12,10},{14... | collective-permute-start | bytes 589832 | tf_op jit(solution)/shard_map/ppermute | solution.py:101
  255.7 7.3 %collective-permute-start.32 = (bf16[128,768]{1,0:T(8,128)(2,1)S(1)}, bf16[128,768]{1,0:T(8,128)(2,1)S(1)}, u32[]{:S(2)}, u32[]{:S(2)}) collective-permute-start(bf16[128,768]{1,0:T(8,128)(2,1)S(1)} %get-tuple-element.13), channel_id=1, source_target_pairs={{0,2},{2,4},{4,6},{6,7},{7,5},{5,3},{3,1},{1,0},{8,10},{10,12},{12... | collective-permute-start | bytes 589832 | tf_op jit(solution)/shard_map/ppermute | solution.py:100
  255.8 7.2 %collective-permute-start.39 = (bf16[128,768]{1,0:T(8,128)(2,1)S(1)}, bf16[128,768]{1,0:T(8,128)(2,1)S(1)}, u32[]{:S(2)}, u32[]{:S(2)}) collective-permute-start(bf16[128,768]{1,0:T(8,128)(2,1)S(1)} %get-tuple-element.14), channel_id=1, source_target_pairs={{2,0},{4,2},{6,4},{7,6},{5,7},{3,5},{1,3},{0,1},{10,8},{12,10},{14... | collective-permute-start | bytes 589832 | tf_op jit(solution)/shard_map/ppermute | solution.py:101
  257.7 53.6 %copy-start.1 = (bf16[1,256,768]{2,1,0:T(8,128)(2,1)S(1)}, bf16[1,256,768]{2,1,0:T(8,128)(2,1)}, u32[]{:S(2)}) copy-start(bf16[1,256,768]{2,1,0:T(8,128)(2,1)} %param.10) | copy-start | bytes 1179652
  257.7 53.6 %copy-start.9 = (s32[1,256,768]{2,1,0:T(8,128)S(1)}, s32[1,256,768]{2,1,0:T(8,128)}, u32[]{:S(2)}) copy-start(s32[1,256,768]{2,1,0:T(8,128)} %param.19) | copy-start | bytes 2359300
  257.7 53.6 %copy-start.10 = (s32[1,256,768]{2,1,0:T(8,128)S(1)}, s32[1,256,768]{2,1,0:T(8,128)}, u32[]{:S(2)}) copy-start(s32[1,256,768]{2,1,0:T(8,128)} %param.18) | copy-start | bytes 2359300
  264.1 6.0 %collective-permute-start.33 = (bf16[128,768]{1,0:T(8,128)(2,1)S(1)}, bf16[128,768]{1,0:T(8,128)(2,1)S(1)}, u32[]{:S(2)}, u32[]{:S(2)}) collective-permute-start(bf16[128,768]{1,0:T(8,128)(2,1)S(1)} %get-tuple-element.11), channel_id=1, source_target_pairs={{0,2},{2,4},{4,6},{6,7},{7,5},{5,3},{3,1},{1,0},{8,10},{10,12},{12... | collective-permute-start | bytes 589832 | tf_op jit(solution)/shard_map/ppermute | solution.py:100
  266.9 5.7 %collective-permute-start.40 = (bf16[128,768]{1,0:T(8,128)(2,1)S(1)}, bf16[128,768]{1,0:T(8,128)(2,1)S(1)}, u32[]{:S(2)}, u32[]{:S(2)}) collective-permute-start(bf16[128,768]{1,0:T(8,128)(2,1)S(1)} %get-tuple-element.12), channel_id=1, source_target_pairs={{2,0},{4,2},{6,4},{7,6},{5,7},{3,5},{1,3},{0,1},{10,8},{12,10},{14... | collective-permute-start | bytes 589832 | tf_op jit(solution)/shard_map/ppermute | solution.py:101
  273.7 15.3 %collective-permute-start.41 = (bf16[256,768]{1,0:T(8,128)(2,1)S(1)}, bf16[256,768]{1,0:T(8,128)(2,1)S(1)}, u32[]{:S(2)}, u32[]{:S(2)}) collective-permute-start(bf16[256,768]{1,0:T(8,128)(2,1)S(1)} %pad_maximum_fusion.13), channel_id=1, source_target_pairs={{0,0},{2,16},{4,8},{6,24},{7,1},{5,17},{3,9},{1,25},{8,10},{10,26}... | collective-permute-start | bytes 1179656 | tf_op jit(solution)/shard_map/ppermute | solution.py:246
  275.6 35.7 %collective-permute-start.18 = (bf16[256,768]{1,0:T(8,128)(2,1)}, bf16[256,768]{1,0:T(8,128)(2,1)S(1)}, u32[]{:S(2)}, u32[]{:S(2)}) collective-permute-start(bf16[256,768]{1,0:T(8,128)(2,1)} %reduce-scatter.2.cloned.1.call-done), channel_id=1, source_target_pairs={{0,0},{1,16},{2,8},{3,24},{4,1},{5,17},{6,9},{7,25},{8,10},{9,26},... | collective-permute-start | bytes 1179656 | tf_op jit(solution)/shard_map/ppermute | solution.py:234
Sparse Core Ops, SparseCore 0:
  162.1 79.3 reduce-scatter.1
where the time goes:
time: 320 us; the launch traced here: 319 us
  waiting for transfers between devices  174 us (54%)
  matrix products  49.5 us (15%)
  starting transfers between devices  42.1 us (13%)
  other arithmetic  25 us (8%)
  between operations  14.4 us (4%)
  local copies, waits for them, and re-layouts  14 us (4%)
    ppermute x14, waiting for transfers between devices, swap(): return lax.ppermute(values, 'gx', [(i, i ^ bit) for i in range(n_gx)])  63.4 us
    dot_general x18, matrix products, mul(): return jnp.dot(left, right, preferred_element_type=f32)  48.8 us
    ppermute x7, waiting for transfers between devices, ring_scatter(): came_up = lax.ppermute(up, 'gy', ahead)  34 us
    ppermute x3, waiting for transfers between devices, ring_gather(): forward.append(lax.ppermute(forward[-1], 'gy', ahead))  24.3 us
    ppermute x1, waiting for transfers between devices, per_device(): lax.ppermute(attention_out, ('gx', 'gy'), home(range(n_gy))).astype(f32)  22.3 us
    ppermute x1, waiting for transfers between devices, per_device(): lax.ppermute(feedforward_out, ('gx', 'gy'), home(ring)).astype(f32)  10.9 us
    unnamed x51, local copies, waits for them, and re-layouts  10.6 us
    ppermute x7, waiting for transfers between devices, ring_scatter(): came_down = lax.ppermute(down, 'gy', back)  10.2 us
  transfers between devices with their start and end apart: 43, of which 27 were waited for; matrix products, arithmetic and copies ran while one was open for 25% of the time, Pallas kernels for 0%

commit v1 on v0

--- a/solution.py
+++ b/solution.py
@@ -1,6 +1,10 @@
+import functools
+
 import jax
 import jax.numpy as jnp
 from jax import lax
+from jax.experimental import pallas as pl
+from jax.experimental.pallas import tpu as pltpu
 from jax.sharding import PartitionSpec as P
 
 epsilon = 1e-06
@@ -252,6 +256,731 @@
     return (tokens.astype(f32) + branches * keep_scale).astype(bf16)
 
 
+MESH = pl.DeviceIdType.MESH
+VMEM_LIMIT = 67043328
+GATHER_PIECES = 2
+ROW_STEP = 64
+
+
+def flip(index, mask):
+    for bit in (1, 2):
+        if mask & bit:
+            index = index + bit - 2 * bit * ((index // bit) % 2)
+    return index
+
+
+def remote(src, dst, send_sem, recv_sem, device):
+    return pltpu.make_async_remote_copy(
+        src_ref=src,
+        dst_ref=dst,
+        send_sem=send_sem,
+        recv_sem=recv_sem,
+        device_id=device,
+        device_id_type=MESH,
+    )
+
+
+def over_rows(count, body):
+    def step(i, carry):
+        body(pl.ds(pl.multiple_of(i * ROW_STEP, ROW_STEP), ROW_STEP))
+        return carry
+
+    lax.fori_loop(0, count // ROW_STEP, step, 0)
+
+
+def aligned(start, size):
+    return pl.ds(pl.multiple_of(start, size), size)
+
+
+def block_kernel(
+    n_gy,
+    tokens,
+    gain,
+    query_gain,
+    key_gain,
+    qkv_hbm,
+    up_hbm,
+    out_hbm,
+    down_hbm,
+    attention_keep,
+    feedforward_keep,
+    result,
+    *scratch,
+):
+    (
+        w_in,
+        w_down,
+        w_out,
+        keeps,
+        stat_own,
+        stat_all,
+        normed,
+        rows_in,
+        part,
+        part_in,
+        kept,
+        cross,
+        cross_in,
+        hid,
+        att,
+        branch,
+        branch_in,
+        line_out,
+        line_low,
+        line_high,
+        running,
+        final,
+        in_sem,
+        down_sem,
+        out_sem,
+        keep_sem,
+        stat_send,
+        stat_recv,
+        first_send,
+        gather_recv,
+        gather_send,
+        side_send,
+        side_recv,
+        part_send,
+        part_recv,
+        cross_send,
+        cross_recv,
+        share_send,
+        share_recv,
+        branch_send,
+        branch_recv,
+        line_send,
+        low_recv,
+        high_recv,
+        final_recv,
+        branch_credit,
+        line_credit,
+    ) = scratch
+    n_gx = 4
+    sub = n_gy // n_gx
+    g, j = lax.axis_index("gx"), lax.axis_index("gy")
+    z, x = j // sub, j % sub
+    core, across, side = (flip(g, 1), j), (flip(g, 2), j), (g, j + 1 - 2 * x)
+    seq, slice_width = normed.shape
+    features = n_gy * slice_width
+    head = query_gain.shape[1]
+    quarter_head, quarter_ff = att.shape[2] // n_gx, hid.shape[2] // n_gx
+    quarter = part.shape[2]
+    chunks = n_gx
+    step_rows = seq // GATHER_PIECES
+    own_cols, side_cols = pl.ds(0, slice_width), pl.ds(slice_width, slice_width)
+
+    relative = (3, 2, 1, 0)
+    in_copies, down_copies, out_copies = [], [], []
+    for q, r in enumerate(relative):
+        k = flip(g, r)
+        copies = []
+        for h in range(2):
+            from_rows = aligned(slice_width * (x if h == 0 else 1 - x), slice_width)
+            to_rows = pl.ds(h * slice_width, slice_width)
+            for t in range(3):
+                copies.append(
+                    (
+                        qkv_hbm.at[t, from_rows, aligned(k * quarter_head, quarter_head)],
+                        w_in.at[q, to_rows, pl.ds(t * quarter_head, quarter_head)],
+                    )
+                )
+            copies.append(
+                (
+                    up_hbm.at[from_rows, aligned(k * quarter_ff, quarter_ff)],
+                    w_in.at[q, to_rows, pl.ds(3 * quarter_head, quarter_ff)],
+                )
+            )
+        in_copies.append(
+            [
+                pltpu.make_async_copy(a, b, in_sem.at[q, n])
+                for n, (a, b) in enumerate(copies)
+            ]
+        )
+    for s in range(2):
+        from_cols = aligned(slice_width * (1 - x if s == 0 else x), slice_width)
+        for r in range(n_gx):
+            k = flip(g, r)
+            down_copies.append(
+                pltpu.make_async_copy(
+                    down_hbm.at[aligned(k * quarter_ff, quarter_ff), from_cols],
+                    w_down.at[s, pl.ds(r * quarter_ff, quarter_ff)],
+                    down_sem.at[s, r],
+                )
+            )
+            out_copies.append(
+                pltpu.make_async_copy(
+                    out_hbm.at[aligned(k * quarter_head, quarter_head), from_cols],
+                    w_out.at[s, pl.ds(r * quarter_head, quarter_head)],
+                    out_sem.at[s, r],
+                )
+            )
+    keep_copies = [
+        pltpu.make_async_copy(attention_keep, keeps.at[0], keep_sem.at[0]),
+        pltpu.make_async_copy(feedforward_keep, keeps.at[1], keep_sem.at[1]),
+    ]
+    for copies in in_copies:
+        for copy in copies:
+            copy.start()
+    for copy in down_copies + out_copies + keep_copies:
+        copy.start()
+
+    barrier = pltpu.get_barrier_semaphore()
+    for r in range(1, n_gx):
+        pl.semaphore_signal(
+            barrier, inc=1, device_id=(flip(g, r), j), device_id_type=MESH
+        )
+    for d in range(1, n_gy):
+        pl.semaphore_signal(
+            barrier, inc=1, device_id=(g, (j + d) % n_gy), device_id_type=MESH
+        )
+
+    wide = tokens[0].astype(f32)
+    mean = jnp.mean(wide, axis=1, keepdims=True)
+    squares = jnp.sum((wide - mean) ** 2, axis=1, keepdims=True)
+    mean_row = jnp.transpose(jnp.broadcast_to(mean, (seq, 128)))[:8]
+    squares_row = jnp.transpose(jnp.broadcast_to(squares, (seq, 128)))[:8]
+    top = lax.broadcasted_iota(jnp.int32, (8, seq), 0) == 0
+    stats = jnp.where(top, mean_row, squares_row)
+    stat_own[...] = stats
+    stat_all[0] = stats
+    pl.semaphore_wait(barrier, n_gx + n_gy - 2)
+    stat_copies = [
+        remote(
+            stat_own,
+            stat_all.at[d],
+            stat_send.at[d],
+            stat_recv.at[d],
+            (g, (j + d) % n_gy),
+        )
+        for d in range(1, n_gy)
+    ]
+    for copy in stat_copies:
+        copy.start()
+    for copy in stat_copies:
+        copy.wait_recv()
+    means = [stat_all[d, 0:1] for d in range(n_gy)]
+    total_mean = sum(means) * (1.0 / n_gy)
+    spread = sum((m - total_mean) ** 2 for m in means) * float(slice_width)
+    spread = spread + sum(stat_all[d, 1:2] for d in range(n_gy))
+    scale = lax.rsqrt(spread * (1.0 / features) + epsilon)
+    mean_col = jnp.transpose(jnp.broadcast_to(total_mean, (128, seq)))
+    scale_col = jnp.transpose(jnp.broadcast_to(scale, (128, seq)))
+    for c0 in range(0, slice_width, 128):
+        cols = slice(c0, c0 + 128)
+        centre = tokens[0, :, cols].astype(f32) - mean_col
+        normed[:, cols] = (centre * scale_col * gain[j, :, cols]).astype(bf16)
+
+    at_root = g == z
+    first_copies = [
+        remote(
+            normed.at[pl.ds(p * step_rows, step_rows)],
+            rows_in.at[g, pl.ds(p * step_rows, step_rows), own_cols],
+            first_send.at[p],
+            gather_recv.at[g, p],
+            (z, j),
+        )
+        for p in range(GATHER_PIECES)
+    ]
+
+    @pl.when(at_root)
+    def _():
+        rows_in[g, :, own_cols] = normed[...]
+
+    @pl.when(jnp.logical_not(at_root))
+    def _():
+        for copy in first_copies:
+            copy.start()
+
+    goes_down = jnp.logical_and(z <= g, z > 0)
+    goes_up = jnp.logical_and(z >= g, z < n_gx - 1)
+
+    def gather_ref(c, p, cols):
+        return rows_in.at[c, pl.ds(p * step_rows, step_rows), cols]
+
+    def gather_copies(c, p):
+        own = gather_ref(c, p, own_cols)
+        down = remote(
+            own, own, gather_send.at[0, c, p], gather_recv.at[c, p], (g, j - sub)
+        )
+        up = remote(
+            own, own, gather_send.at[1, c, p], gather_recv.at[c, p], (g, j + sub)
+        )
+        beside = remote(
+            own,
+            gather_ref(c, p, side_cols),
+            side_send.at[c, p],
+            side_recv.at[c, p],
+            side,
+        )
+        return down, up, beside
+
+    def gather(c):
+        for p in range(GATHER_PIECES):
+            down, up, beside = gather_copies(c, p)
+
+            @pl.when(jnp.logical_not(jnp.logical_and(at_root, g == c)))
+            def _():
+                up.wait_recv()
+
+            @pl.when(goes_up)
+            def _():
+                up.start()
+
+            @pl.when(goes_down)
+            def _():
+                down.start()
+
+            beside.start()
+
+    def gathered(c):
+        for p in range(GATHER_PIECES):
+            gather_copies(c, p)[2].wait_recv()
+
+    def part_copy(c, half):
+        return remote(
+            part.at[2 * half],
+            part_in.at[c % 2, half],
+            part_send.at[c, half],
+            part_recv.at[c, half],
+            core,
+        )
+
+    def cross_copy(c):
+        return remote(
+            cross.at[c % 2], cross_in.at[c], cross_send.at[c], cross_recv.at[c], across
+        )
+
+    def project(c, half):
+        if c == 0:
+            for copy in in_copies[2 * half] + in_copies[2 * half + 1]:
+                copy.wait()
+        else:
+            part_copy(c - 1, half).wait_send()
+
+        def one(i, carry):
+            q = 2 * half + i
+            for n0 in range(0, quarter, 256):
+                n1 = min(n0 + 256, quarter)
+                part[q, :, n0:n1] = mul(rows_in[c], w_in[q, :, n0:n1]).astype(bf16)
+
+            @pl.when(i == 0)
+            def _():
+                part_copy(c, half).start()
+
+            return carry
+
+        lax.fori_loop(0, 2, one, 0)
+
+    def exchange(c):
+        gathered(c)
+        project(c, 0)
+        part_copy(c, 0).wait_recv()
+        if c >= 2:
+            cross_copy(c - 2).wait_send()
+
+        def to_cross(rows):
+            total = part[1, rows].astype(f32) + part_in[c % 2, 0, rows].astype(f32)
+            cross[c % 2, rows] = total.astype(bf16)
+
+        over_rows(seq, to_cross)
+        cross_copy(c).start()
+        project(c, 1)
+        part_copy(c, 1).wait_recv()
+
+        def to_kept(rows):
+            kept[c % 2, rows] = part[3, rows].astype(f32) + part_in[
+                c % 2, 1, rows
+            ].astype(f32)
+
+        over_rows(seq, to_kept)
+
+    def share_copies(c, which):
+        held, width = (hid, quarter_ff) if which == 0 else (att, quarter_head)
+
+        def slot(r):
+            return held.at[c, :, pl.ds(r * width, width)]
+
+        return [
+            remote(
+                slot(a),
+                slot(b),
+                share_send.at[c, which, n],
+                share_recv.at[c, which, n],
+                device,
+            )
+            for n, (a, b, device) in enumerate(
+                ((0, 2, across), (0, 1, core), (2, 3, core))
+            )
+        ]
+
+    def activate(c):
+        cross_copy(c).wait_recv()
+        first = 3 * quarter_head
+
+        def to_hidden(rows):
+            total = kept[c % 2, rows, first:] + cross_in[c, rows, first:].astype(f32)
+            hid[c, rows, 0:quarter_ff] = (
+                0.5 * total * (1.0 + lax.erf(total * (0.5**0.5)))
+            ).astype(bf16)
+
+        over_rows(seq, to_hidden)
+        to_across, to_core, _ = share_copies(c, 0)
+        to_across.start()
+        to_core.start()
+        for h in range(quarter_head // head):
+
+            def of(t):
+                cols = slice(t * quarter_head + h * head, t * quarter_head + (h + 1) * head)
+                return kept[c % 2, :, cols] + cross_in[c, :, cols].astype(f32)
+
+            query = layer_norm(of(0), query_gain[...]).astype(bf16)
+            key = layer_norm(of(1), key_gain[...]).astype(bf16)
+            value = of(2).astype(bf16)
+            scores = lax.dot_general(
+                query, key, (((1,), (1,)), ((), ())), preferred_element_type=f32
+            ) * head ** (-0.5)
+            raised = jnp.exp(scores)
+            weights = (raised / jnp.sum(raised, axis=-1, keepdims=True)).astype(bf16)
+            att[c, :, h * head : (h + 1) * head] = mul(weights, value).astype(bf16)
+        to_across, to_core, _ = share_copies(c, 1)
+        to_across.start()
+        to_core.start()
+
+    def forward(c):
+        for which in range(2):
+            from_across, _, onward = share_copies(c, which)
+            from_across.wait_recv()
+            onward.start()
+
+    def branch_copy(p):
+        c, b = p // 2, p % 2
+        return remote(
+            branch.at[c % 2, b, 0],
+            branch_in.at[p % 4],
+            branch_send.at[p],
+            branch_recv.at[p],
+            side,
+        )
+
+    def finish(c):
+        for which, held, weight, copies in (
+            (1, att, w_out, out_copies),
+            (0, hid, w_down, down_copies),
+        ):
+            _, from_core, onward = share_copies(c, which)
+            from_core.wait_recv()
+            onward.wait_recv()
+            if c == 0:
+                for copy in copies:
+                    copy.wait()
+            b = 1 - which
+            p = 2 * c + b
+            if p >= 4:
+                branch_copy(p - 4).wait_send()
+
+            def one(s, carry):
+                for n0 in range(0, slice_width, 256):
+                    n1 = min(n0 + 256, slice_width)
+                    branch[c % 2, b, s, :, n0:n1] = mul(
+                        held[c], weight[s, :, n0:n1]
+                    ).astype(bf16)
+
+                @pl.when(s == 0)
+                def _():
+                    if p >= 4:
+                        pl.semaphore_wait(branch_credit, 1)
+                    branch_copy(p).start()
+
+                return carry
+
+            lax.fori_loop(0, 2, one, 0)
+
+    from_low = jnp.logical_and(z <= g, z > 0)
+    from_high = jnp.logical_and(z >= g, z < n_gx - 1)
+    below, above = z < g, z > g
+
+    def line_copies(p):
+        c, b = p // 2, p % 2
+        k = p % 4
+        up = remote(
+            line_out.at[k], line_low.at[k], line_send.at[p], low_recv.at[p], (g, j + sub)
+        )
+        down = remote(
+            line_out.at[k],
+            line_high.at[k],
+            line_send.at[p],
+            high_recv.at[p],
+            (g, j - sub),
+        )
+        home = remote(
+            line_out.at[k], final.at[b], line_send.at[p], final_recv.at[b], (c, j)
+        )
+        return up, down, home
+
+    def leaves(p):
+        return jnp.logical_not(jnp.logical_and(at_root, g == p // 2))
+
+    def reduce(p):
+        c, b = p // 2, p % 2
+        k = p % 4
+        up, down, home = line_copies(p)
+        branch_copy(p).wait_recv()
+
+        def begin(rows):
+            running[rows] = branch[c % 2, b, 1, rows].astype(f32) + branch_in[
+                k, rows
+            ].astype(f32)
+
+        over_rows(seq, begin)
+        if p < 4:
+            pl.semaphore_signal(
+                branch_credit, inc=1, device_id=side, device_id_type=MESH
+            )
+        for here, copy, held, source in (
+            (from_low, up, line_low, (g, j - sub)),
+            (from_high, down, line_high, (g, j + sub)),
+        ):
+
+            @pl.when(here)
+            def _():
+                copy.wait_recv()
+
+                def add(rows):
+                    running[rows] = running[rows] + held[k, rows].astype(f32)
+
+                over_rows(seq, add)
+                if p < 4:
+                    pl.semaphore_signal(
+                        line_credit, inc=1, device_id=source, device_id_type=MESH
+                    )
+
+        if p >= 4:
+
+            @pl.when(leaves(p - 4))
+            def _():
+                line_copies(p - 4)[0].wait_send()
+
+            @pl.when(jnp.logical_not(at_root))
+            def _():
+                pl.semaphore_wait(line_credit, 1)
+
+        def settle(rows):
+            line_out[k, rows] = running[rows].astype(bf16)
+
+        over_rows(seq, settle)
+
+        @pl.when(below)
+        def _():
+            up.start()
+
+        @pl.when(above)
+        def _():
+            down.start()
+
+        @pl.when(at_root)
+        def _():
+            @pl.when(g == c)
+            def _():
+                final[b] = line_out[k]
+
+            @pl.when(g != c)
+            def _():
+                home.start()
+
+    gather(0)
+    exchange(0)
+    gather(1)
+    exchange(1)
+    gather(2)
+    gather(3)
+    activate(0)
+    exchange(2)
+    activate(1)
+    forward(0)
+    finish(0)
+    exchange(3)
+    activate(2)
+    reduce(0)
+    reduce(1)
+    forward(1)
+    finish(1)
+    activate(3)
+    reduce(2)
+    reduce(3)
+    forward(2)
+    finish(2)
+    forward(3)
+    finish(3)
+    for p in range(4, 8):
+        reduce(p)
+
+    for copy in keep_copies:
+        copy.wait()
+
+    @pl.when(jnp.logical_not(at_root))
+    def _():
+        for b in range(2):
+            line_copies(b)[2].wait_recv()
+
+    def last(rows):
+        total = keeps[0, 0, rows].astype(f32) * final[0, rows].astype(f32)
+        total = total + keeps[1, 0, rows].astype(f32) * final[1, rows].astype(f32)
+        result[0, rows] = (tokens[0, rows].astype(f32) + total * keep_scale).astype(
+            bf16
+        )
+
+    over_rows(seq, last)
+
+    for copy in stat_copies:
+        copy.wait_send()
+
+    @pl.when(jnp.logical_not(at_root))
+    def _():
+        for copy in first_copies:
+            copy.wait_send()
+
+    for c in range(chunks):
+        for p in range(GATHER_PIECES):
+            down, up, beside = gather_copies(c, p)
+            beside.wait_send()
+
+            @pl.when(goes_up)
+            def _():
+                up.wait_send()
+
+            @pl.when(goes_down)
+            def _():
+                down.wait_send()
+
+        for which in range(2):
+            for copy in share_copies(c, which):
+                copy.wait_send()
+    for half in range(2):
+        part_copy(chunks - 1, half).wait_send()
+    for c in range(chunks - 2, chunks):
+        cross_copy(c).wait_send()
+    for p in range(4, 8):
+        branch_copy(p).wait_send()
+
+        @pl.when(leaves(p))
+        def _():
+            line_copies(p)[0].wait_send()
+
+
+def fused(
+    tokens,
+    norm_gain,
+    qkv_weight,
+    up_weight,
+    query_gain,
+    key_gain,
+    out_weight,
+    down_weight,
+    attention_keep,
+    feedforward_keep,
+):
+    n_gx, n_gy = lax.axis_size("gx"), lax.axis_size("gy")
+    _, seq, slice_width = tokens.shape
+    block_width, _, head_cols = qkv_weight.shape
+    ff_cols = up_weight.shape[1]
+    head = query_gain.shape[0]
+    quarter_head, quarter_ff = head_cols // n_gx, ff_cols // n_gx
+    quarter = 3 * quarter_head + quarter_ff
+    chunks, pieces = n_gx, 2 * n_gx
+    dma, vmem = pltpu.SemaphoreType.DMA, pltpu.VMEM
+    scratch = [
+        vmem((n_gx, block_width, quarter), bf16),
+        vmem((2, ff_cols, slice_width), bf16),
+        vmem((2, head_cols, slice_width), bf16),
+        vmem((2, 1, seq, slice_width), jnp.int32),
+        vmem((8, seq), f32),
+        vmem((n_gy, 8, seq), f32),
+        vmem((seq, slice_width), bf16),
+        vmem((chunks, seq, block_width), bf16),
+        vmem((n_gx, seq, quarter), bf16),
+        vmem((2, 2, seq, quarter), bf16),
+        vmem((2, seq, quarter), f32),
+        vmem((2, seq, quarter), bf16),
+        vmem((chunks, seq, quarter), bf16),
+        vmem((chunks, seq, ff_cols), bf16),
+        vmem((chunks, seq, head_cols), bf16),
+        vmem((2, 2, 2, seq, slice_width), bf16),
+        vmem((4, seq, slice_width), bf16),
+        vmem((4, seq, slice_width), bf16),
+        vmem((4, seq, slice_width), bf16),
+        vmem((4, seq, slice_width), bf16),
+        vmem((seq, slice_width), f32),
+        vmem((2, seq, slice_width), bf16),
+        dma((n_gx, 8)),
+        dma((2, n_gx)),
+        dma((2, n_gx)),
+        dma((2,)),
+        dma((n_gy,)),
+        dma((n_gy,)),
+        dma((GATHER_PIECES,)),
+        dma((chunks, GATHER_PIECES)),
+        dma((2, chunks, GATHER_PIECES)),
+        dma((chunks, GATHER_PIECES)),
+        dma((chunks, GATHER_PIECES)),
+        dma((chunks, 2)),
+        dma((chunks, 2)),
+        dma((chunks,)),
+        dma((chunks,)),
+        dma((chunks, 2, 3)),
+        dma((chunks, 2, 3)),
+        dma((pieces,)),
+        dma((pieces,)),
+        dma((pieces,)),
+        dma((pieces,)),
+        dma((pieces,)),
+        dma((2,)),
+        pltpu.SemaphoreType.REGULAR,
+        pltpu.SemaphoreType.REGULAR,
+    ]
+    in_vmem = pl.BlockSpec(memory_space=pltpu.VMEM)
+    anywhere = pl.BlockSpec(memory_space=pl.ANY)
+    return pl.pallas_call(
+        functools.partial(block_kernel, n_gy),
+        out_shape=jax.ShapeDtypeStruct(tokens.shape, bf16),
+        in_specs=[in_vmem] * 4 + [anywhere] * 6,
+        out_specs=in_vmem,
+        scratch_shapes=scratch,
+        compiler_params=pltpu.CompilerParams(
+            collective_id=0, has_side_effects=True, vmem_limit_bytes=VMEM_LIMIT
+        ),
+    )(
+        tokens,
+        norm_gain.reshape(n_gy, 1, slice_width),
+        query_gain.reshape(1, head),
+        key_gain.reshape(1, head),
+        jnp.transpose(qkv_weight, (1, 0, 2)),
+        up_weight,
+        out_weight,
+        down_weight,
+        attention_keep,
+        feedforward_keep,
+    )
+
+
+def dispatch(*arrays):
+    n_gx, n_gy = lax.axis_size("gx"), lax.axis_size("gy")
+    images, seq, slice_width = arrays[0].shape
+    head_cols, ff_cols = arrays[2].shape[2], arrays[3].shape[1]
+    head = arrays[4].shape[0]
+    fits = (
+        n_gx == 4
+        and n_gy == 2 * n_gx
+        and images == 1
+        and head == 128
+        and head_cols % (n_gx * head) == 0
+        and ff_cols % (n_gx * 128) == 0
+        and slice_width % 128 == 0
+        and seq % 128 == 0
+    )
+    return fused(*arrays) if fits else per_device(*arrays)
+
+
 def solution(mesh):
     in_specs = (
         P("gx", None, "gy"),
@@ -267,5 +996,5 @@
     )
     out_specs = P("gx", None, "gy")
     return jax.shard_map(
-        per_device, mesh=mesh, in_specs=in_specs, out_specs=out_specs, check_vma=False
+        dispatch, mesh=mesh, in_specs=in_specs, out_specs=out_specs, check_vma=False
     )

time: 320 us -> 212 us (0.66)
  Pallas kernels: 0 us -> 209 us
  waiting for transfers between devices: 174 us -> 0 us
  matrix products: 49.5 us -> 0 us
  starting transfers between devices: 42.1 us -> 0 us
  other arithmetic: 25 us -> 0 us
  between operations: 14.4 us -> 0.01 us
  local copies, waits for them, and re-layouts: 14 us -> 1.77 us
    pallas_call x0 -> x1, Pallas kernels: none -> 209 us  [fused(): pl.pallas_call(functools.partial(block_kernel, n_gy), out_shape=jax.Shape...]
    ppermute x42 -> x0, waiting for transfers between devices: 174 us -> none  [the longest x14 63.4 us: swap(): return lax.ppermute(values, 'gx', [(i, i ^ bit) for i in range(n_gx)])]
    dot_general x20 -> x0, matrix products: 49.5 us -> none  [the longest x18 48.8 us: mul(): return jnp.dot(left, right, preferred_element_type=f32)]
    ppermute x42 -> x0, starting transfers between devices: 42.1 us -> none  [the longest x7 7.89 us: ring_scatter(): came_up = lax.ppermute(up, 'gy', ahead)]
    convert_element_type x12 -> x0, other arithmetic: 19.7 us -> none  [the longest x2 9.24 us: per_device(): hidden.append(jax.nn.gelu(total, approximate=False).astype(bf16))]
    unnamed x51 -> x1, local copies, waits for them, and re-layouts: 10.6 us -> 1.77 us
  transfers between devices with their start and end apart: 43 -> 0, of which waited for: 27 -> 0; matrix products, arithmetic and copies ran while one was open for 25% -> 0% of each run, Pallas kernels for 0% -> 0%
where the time goes in v1:
time: 212 us; the launch traced here: 210 us
  Pallas kernels  209 us (99%)
    pallas_call x1, Pallas kernels, fused(): pl.pallas_call(functools.partial(block_kernel, n_gy), out_shape=jax.Shape...  209 us

profile of v1, /device:TPU:2, one launch (start us, length us, event | category | flops | bytes accessed | tf_op | source)
XLA Modules:
  0.0 210.4 jit_solution(8667680150615740980)
XLA Ops:
  0.0 208.6 %shard_map.100 = bf16[1,256,768]{2,1,0:T(8,128)(2,1)} custom-call(bf16[1,256,768]{2,1,0:T(8,128)(2,1)} %tokens.1, f32[8,1,768]{2,1,0:T(1,128)} %bitcast.5, f32[1,128]{1,0:T(1,128)} %bitcast.6, f32[1,128]{1,0:T(1,128)} %bitcast.7, bf16[3,1536,512]{2,1,0:T(8,128)(2,1)} %bitcast.4, bf16[1536,3072]{1,0:T(8,128)(2,1)} %up_hbm.1, bf16[512,1536]{1,0:T(8,128)(2,1)} %out_hbm.1, ...), custom_call_target="tpu_custom_call" | custom-call | tf_op jit(solution)/shard_map/pallas_call | solution.py:943
  208.6 1.8 copy.12

commit v2 on v1

--- a/solution.py
+++ b/solution.py
@@ -258,8 +258,9 @@
 
 MESH = pl.DeviceIdType.MESH
 VMEM_LIMIT = 67043328
-GATHER_PIECES = 2
+GATHER_PIECES = 4
 ROW_STEP = 64
+FIRST_SECTIONS = 1
 
 
 def flip(index, mask):
@@ -267,6 +268,25 @@
         if mask & bit:
             index = index + bit - 2 * bit * ((index // bit) % 2)
     return index
+
+
+SCHEDULE = (
+    "mark0", "relay0", "relay1", "relay2/root", "relay3/root", "gather0", "exchange0",
+    "relay2/mid", "exchange1", "masks0/root", "relay3/mid", "activate0",
+    "masks1/root", "gather3", "exchange2", "activate1", "masks0/near", "forward0", "finish0",
+    "masks1/near", "reduce0/0", "activate2", "exchange3", "masks0/far", "reduce1/0",
+    "reduce0/1", "forward1", "finish1", "masks1/far", "reduce1/1", "reduce0/2", "forward2",
+    "finish2", "reduce2/0", "reduce3/0", "reduce1/2", "activate3", "reduce2/1", "reduce0/3",
+    "reduce1/3", "reduce4/0", "reduce3/1", "forward3", "masks0/end", "masks1/end",
+    "finish3", "reduce5/0", "close3", "reduce2/2", "reduce3/2", "reduce2/3", "reduce3/3", "reduce4/late",
+    "reduce5/late", "reduce6", "reduce7",
+)
+
+
+def schedule():
+    for word in SCHEDULE:
+        name, _, role = word.partition("/")
+        yield name[:-1], int(name[-1]), role
 
 
 def remote(src, dst, send_sem, recv_sem, device):
@@ -278,6 +298,9 @@
         device_id=device,
         device_id_type=MESH,
     )
+
+
+scope = jax.named_scope
 
 
 def over_rows(count, body):
@@ -324,12 +347,14 @@
         hid,
         att,
         branch,
+        merged,
         branch_in,
         line_out,
         line_low,
         line_high,
-        running,
         final,
+        mask_own,
+        mask_in,
         in_sem,
         down_sem,
         out_sem,
@@ -353,8 +378,12 @@
         low_recv,
         high_recv,
         final_recv,
-        branch_credit,
+        mask_first,
+        mask_recv,
+        mask_send,
+        mask_side,
         line_credit,
+        turn,
     ) = scratch
     n_gx = 4
     sub = n_gy // n_gx
@@ -419,6 +448,8 @@
         pltpu.make_async_copy(attention_keep, keeps.at[0], keep_sem.at[0]),
         pltpu.make_async_copy(feedforward_keep, keeps.at[1], keep_sem.at[1]),
     ]
+    mark_scope = scope('begin')
+    mark_scope.__enter__()
     for copies in in_copies:
         for copy in copies:
             copy.start()
@@ -435,6 +466,9 @@
             barrier, inc=1, device_id=(g, (j + d) % n_gy), device_id_type=MESH
         )
 
+    mark_scope.__exit__(None, None, None)
+    mark_scope = scope('moments')
+    mark_scope.__enter__()
     wide = tokens[0].astype(f32)
     mean = jnp.mean(wide, axis=1, keepdims=True)
     squares = jnp.sum((wide - mean) ** 2, axis=1, keepdims=True)
@@ -444,7 +478,13 @@
     stats = jnp.where(top, mean_row, squares_row)
     stat_own[...] = stats
     stat_all[0] = stats
+    mark_scope.__exit__(None, None, None)
+    mark_scope = scope('barrier')
+    mark_scope.__enter__()
     pl.semaphore_wait(barrier, n_gx + n_gy - 2)
+    mark_scope.__exit__(None, None, None)
+    mark_scope = scope('swap')
+    mark_scope.__enter__()
     stat_copies = [
         remote(
             stat_own,
@@ -459,6 +499,9 @@
         copy.start()
     for copy in stat_copies:
         copy.wait_recv()
+    mark_scope.__exit__(None, None, None)
+    mark_scope = scope('norm')
+    mark_scope.__enter__()
     means = [stat_all[d, 0:1] for d in range(n_gy)]
     total_mean = sum(means) * (1.0 / n_gy)
     spread = sum((m - total_mean) ** 2 for m in means) * float(slice_width)
@@ -487,13 +530,98 @@
     def _():
         rows_in[g, :, own_cols] = normed[...]
 
+    mark_scope.__exit__(None, None, None)
+    @pl.when(g % 2 == 1)
+    def _():
+        pl.semaphore_wait(turn, 1)
+
     @pl.when(jnp.logical_not(at_root))
     def _():
         for copy in first_copies:
             copy.start()
 
+    @pl.when(g % 2 == 0)
+    def _():
+        @pl.when(jnp.logical_not(at_root))
+        def _():
+            for copy in first_copies:
+                copy.wait_send()
+
+        pl.semaphore_signal(turn, inc=1, device_id=core, device_id_type=MESH)
+
+    join = chunks - 1
+    half_rows = seq // 2
+
+    def mask_ref(i):
+        return mask_in.at[i // 4, i // 2 % 2, pl.ds(i % 2 * half_rows, half_rows)]
+
+    def mask_first_copy(i):
+        return remote(
+            mask_own.at[i // 2, pl.ds(i % 2 * half_rows, half_rows)],
+            mask_ref(i),
+            mask_first.at[i],
+            mask_recv.at[i],
+            (z, j),
+        )
+
+    def mark(_):
+        @pl.when(g >= join)
+        def _():
+            for b in range(2):
+                keep_copies[b].wait()
+
+                def to_mask(rows):
+                    mask_own[b, rows] = keeps[b, 0, rows].astype(f32).astype(bf16)
+
+                over_rows(seq, to_mask)
+
+            @pl.when(at_root)
+            def _():
+                mask_in[0] = mask_own[...]
+
+            @pl.when(jnp.logical_not(at_root))
+            def _():
+                for i in range(4):
+                    mask_first_copy(i).start()
+
     goes_down = jnp.logical_and(z <= g, z > 0)
     goes_up = jnp.logical_and(z >= g, z < n_gx - 1)
+    duty = jnp.logical_or(goes_down, goes_up)
+
+    def mask_copies(i):
+        own = mask_ref(i)
+        down = remote(own, own, mask_send.at[0, i], mask_recv.at[i], (g, j - sub))
+        up = remote(own, own, mask_send.at[1, i], mask_recv.at[i], (g, j + sub))
+        return down, up
+
+    def mask_beside(i):
+        return remote(
+            mask_ref(i), mask_ref(4 + i), mask_side.at[i], mask_recv.at[4 + i], side
+        )
+
+    def masks(s):
+        for i in range(4 * s, 4 * s + 4):
+            down, up = mask_copies(i)
+            if s == 0:
+
+                @pl.when(jnp.logical_not(jnp.logical_and(at_root, g == join)))
+                def _():
+                    up.wait_recv()
+
+                @pl.when(at_root)
+                def _():
+                    mask_beside(i).start()
+
+            else:
+                up.wait_recv()
+
+            @pl.when(goes_up)
+            def _():
+                up.start()
+
+            @pl.when(goes_down)
+            def _():
+                down.start()
 
     def gather_ref(c, p, cols):
         return rows_in.at[c, pl.ds(p * step_rows, step_rows), cols]
@@ -515,8 +643,8 @@
         )
         return down, up, beside
 
-    def gather(c):
-        for p in range(GATHER_PIECES):
+    def gather(c, pieces=range(GATHER_PIECES)):
+        for p in pieces:
             down, up, beside = gather_copies(c, p)
 
             @pl.when(jnp.logical_not(jnp.logical_and(at_root, g == c)))
@@ -533,80 +661,120 @@
 
             beside.start()
 
-    def gathered(c):
-        for p in range(GATHER_PIECES):
+    def gathered(c, pieces):
+        for p in pieces:
             gather_copies(c, p)[2].wait_recv()
 
-    def part_copy(c, half):
+    def sections(c):
+        count = FIRST_SECTIONS if c == 0 else 1
+        return [
+            (sec, slice(sec * seq // count, (sec + 1) * seq // count))
+            for sec in range(count)
+        ]
+
+    def part_copy(c, half, section):
+        sec, rows = section
         return remote(
-            part.at[2 * half],
-            part_in.at[c % 2, half],
-            part_send.at[c, half],
-            part_recv.at[c, half],
+            part.at[2 * half, rows],
+            part_in.at[c % 2, half, rows],
+            part_send.at[c, half, sec],
+            part_recv.at[c, half, sec],
             core,
         )
 
-    def cross_copy(c):
+    def cross_copy(c, section):
+        sec, rows = section
         return remote(
-            cross.at[c % 2], cross_in.at[c], cross_send.at[c], cross_recv.at[c], across
-        )
-
-    def project(c, half):
-        if c == 0:
+            cross.at[c % 2, rows],
+            cross_in.at[c, rows],
+            cross_send.at[c, sec],
+            cross_recv.at[c, sec],
+            across,
+        )
+
+    def project(c, half, section):
+        rows = section[1]
+        if c == 0 and section[0] == 0:
             for copy in in_copies[2 * half] + in_copies[2 * half + 1]:
                 copy.wait()
-        else:
-            part_copy(c - 1, half).wait_send()
+        if c > 0:
+            for earlier in sections(c - 1):
+                part_copy(c - 1, half, earlier).wait_send()
 
         def one(i, carry):
             q = 2 * half + i
             for n0 in range(0, quarter, 256):
                 n1 = min(n0 + 256, quarter)
-                part[q, :, n0:n1] = mul(rows_in[c], w_in[q, :, n0:n1]).astype(bf16)
+                part[q, rows, n0:n1] = mul(
+                    rows_in[c, rows], w_in[q, :, n0:n1]
+                ).astype(bf16)
 
             @pl.when(i == 0)
             def _():
-                part_copy(c, half).start()
+                part_copy(c, half, section).start()
 
             return carry
 
         lax.fori_loop(0, 2, one, 0)
 
     def exchange(c):
-        gathered(c)
-        project(c, 0)
-        part_copy(c, 0).wait_recv()
+        if c >= slots:
+            for unit in range(3):
+                share_copies(c - slots, unit)[2].wait_send()
         if c >= 2:
-            cross_copy(c - 2).wait_send()
-
-        def to_cross(rows):
-            total = part[1, rows].astype(f32) + part_in[c % 2, 0, rows].astype(f32)
-            cross[c % 2, rows] = total.astype(bf16)
-
-        over_rows(seq, to_cross)
-        cross_copy(c).start()
-        project(c, 1)
-        part_copy(c, 1).wait_recv()
-
-        def to_kept(rows):
-            kept[c % 2, rows] = part[3, rows].astype(f32) + part_in[
-                c % 2, 1, rows
-            ].astype(f32)
-
-        over_rows(seq, to_kept)
-
-    def share_copies(c, which):
-        held, width = (hid, quarter_ff) if which == 0 else (att, quarter_head)
+            for earlier in sections(c - 2):
+                cross_copy(c - 2, earlier).wait_send()
+        for section in sections(c):
+            rows = section[1]
+            pieces = range(rows.start // step_rows, rows.stop // step_rows)
+            gathered(c, pieces)
+            project(c, 0, section)
+            part_copy(c, 0, section).wait_recv()
+
+            def to_cross(step):
+                here = pl.ds(rows.start + step.start, ROW_STEP)
+                total = part[1, here].astype(f32) + part_in[c % 2, 0, here].astype(f32)
+                cross[c % 2, here] = total.astype(bf16)
+
+            over_rows(rows.stop - rows.start, to_cross)
+            cross_copy(c, section).start()
+            half_pieces = GATHER_PIECES // 2
+            if c < 2:
+                early = range(half_pieces)
+                pl.when(jnp.logical_not(duty))(functools.partial(gather, c + 1, early))
+            project(c, 1, section)
+            if c < 2:
+                late = range(half_pieces, GATHER_PIECES)
+                pl.when(jnp.logical_not(duty))(functools.partial(gather, c + 1, late))
+            part_copy(c, 1, section).wait_recv()
+
+            def to_kept(step):
+                here = pl.ds(rows.start + step.start, ROW_STEP)
+                kept[c % 2, here] = part[3, here].astype(f32) + part_in[
+                    c % 2, 1, here
+                ].astype(f32)
+
+            over_rows(rows.stop - rows.start, to_kept)
+
+    slots = hid.shape[0]
+    half_rows = seq // 2
+
+    def half_of(h):
+        return slice(h * half_rows, (h + 1) * half_rows)
+
+    def share_copies(c, unit):
+        held, width = (hid, quarter_ff) if unit < 2 else (att, quarter_head)
+        rows = half_of(unit) if unit < 2 else slice(0, seq)
 
         def slot(r):
-            return held.at[c, :, pl.ds(r * width, width)]
+            return held.at[c % slots, rows, pl.ds(r * width, width)]
 
         return [
             remote(
                 slot(a),
                 slot(b),
-                share_send.at[c, which, n],
-                share_recv.at[c, which, n],
+                share_send.at[c, unit, n],
+                share_recv.at[c, unit, n],
                 device,
             )
             for n, (a, b, device) in enumerate(
@@ -614,20 +782,39 @@
             )
         ]
 
+    def share(c, unit):
+        to_across, to_core, _ = share_copies(c, unit)
+        to_across.start()
+        to_core.start()
+
     def activate(c):
-        cross_copy(c).wait_recv()
+        if c >= slots:
+            for unit in range(3):
+                for copy in share_copies(c - slots, unit)[:2]:
+                    copy.wait_send()
+        for section in sections(c):
+            cross_copy(c, section).wait_recv()
+        order = (2, 0, 1) if c >= join else (0, 1, 2)
+        for unit in order:
+            if unit == 2:
+                attend(c)
+            else:
+                activate_rows(c, unit * half_rows)
+            share(c, unit)
+
+    def activate_rows(c, offset):
         first = 3 * quarter_head
 
-        def to_hidden(rows):
+        def to_hidden(step):
+            rows = pl.ds(offset + step.start, ROW_STEP)
             total = kept[c % 2, rows, first:] + cross_in[c, rows, first:].astype(f32)
-            hid[c, rows, 0:quarter_ff] = (
+            hid[c % slots, rows, 0:quarter_ff] = (
                 0.5 * total * (1.0 + lax.erf(total * (0.5**0.5)))
             ).astype(bf16)
 
-        over_rows(seq, to_hidden)
-        to_across, to_core, _ = share_copies(c, 0)
-        to_across.start()
-        to_core.start()
+        over_rows(half_rows, to_hidden)
+
+    def attend(c):
         for h in range(quarter_head // head):
 
             def of(t):
@@ -642,133 +829,179 @@
             ) * head ** (-0.5)
             raised = jnp.exp(scores)
             weights = (raised / jnp.sum(raised, axis=-1, keepdims=True)).astype(bf16)
-            att[c, :, h * head : (h + 1) * head] = mul(weights, value).astype(bf16)
-        to_across, to_core, _ = share_copies(c, 1)
-        to_across.start()
+            att[c % slots, :, h * head : (h + 1) * head] = mul(weights, value).astype(
+                bf16
+            )
+
+    def onward(c, unit):
+        from_across, _, to_core = share_copies(c, unit)
+        from_across.wait_recv()
         to_core.start()
 
     def forward(c):
-        for which in range(2):
-            from_across, _, onward = share_copies(c, which)
-            from_across.wait_recv()
-            onward.start()
+        for unit in (2, 0) if c >= join else (0, 1, 2):
+            onward(c, unit)
+
+    quarter_rows = seq // 4
+
+    def piece_rows(p):
+        if p // 4 < join:
+            return slice(p % 2 * half_rows, (p % 2 + 1) * half_rows)
+        return slice(p % 4 * quarter_rows, (p % 4 + 1) * quarter_rows)
+
+    def piece_slot(p):
+        return p // 2 if p // 4 < join else 2 * join
+
+    def line_slot(p):
+        return p // 2 % 4
+
+    def line_rows(p):
+        rows = piece_rows(p)
+        start = p % 2 * half_rows
+        return slice(start, start + rows.stop - rows.start)
+
+    def branch_ref(p, s):
+        c, b, rows = p // 4, p // 2 % 2, piece_rows(p)
+        return branch.at[c, b, s, rows] if c < join else merged.at[s, rows]
 
     def branch_copy(p):
-        c, b = p // 2, p % 2
         return remote(
-            branch.at[c % 2, b, 0],
-            branch_in.at[p % 4],
+            branch_ref(p, 0),
+            branch_in.at[piece_slot(p), piece_rows(p)],
             branch_send.at[p],
             branch_recv.at[p],
             side,
         )
 
+    def shares_arrive(c, unit):
+        for copy in share_copies(c, unit)[1:]:
+            copy.wait_recv()
+        if c == 0 and unit > 0:
+            for copy in (down_copies, out_copies)[unit - 1]:
+                copy.wait()
+
     def finish(c):
-        for which, held, weight, copies in (
-            (1, att, w_out, out_copies),
-            (0, hid, w_down, down_copies),
-        ):
-            _, from_core, onward = share_copies(c, which)
-            from_core.wait_recv()
-            onward.wait_recv()
-            if c == 0:
-                for copy in copies:
-                    copy.wait()
-            b = 1 - which
-            p = 2 * c + b
-            if p >= 4:
-                branch_copy(p - 4).wait_send()
+        if c >= join:
+            finish_joined(c, 0)
+            onward(c, 1)
+            return
+        for b, held, weight in ((0, att, w_out), (1, hid, w_down)):
+            for unit in (2,) if b == 0 else (0, 1):
+                shares_arrive(c, unit)
 
             def one(s, carry):
                 for n0 in range(0, slice_width, 256):
                     n1 = min(n0 + 256, slice_width)
-                    branch[c % 2, b, s, :, n0:n1] = mul(
-                        held[c], weight[s, :, n0:n1]
+                    branch[c, b, s, :, n0:n1] = mul(
+                        held[c % slots], weight[s, :, n0:n1]
                     ).astype(bf16)
 
                 @pl.when(s == 0)
                 def _():
-                    if p >= 4:
-                        pl.semaphore_wait(branch_credit, 1)
-                    branch_copy(p).start()
+                    for h in range(2):
+                        branch_copy(4 * c + 2 * b + h).start()
 
                 return carry
 
             lax.fori_loop(0, 2, one, 0)
+
+    def finish_joined(c, h):
+        if h == 0:
+            shares_arrive(c, 2)
+        shares_arrive(c, h)
+        rows = half_of(h)
+
+        def one(s, carry):
+            for n0 in range(0, slice_width, 256):
+                cols = slice(n0, min(n0 + 256, slice_width))
+                keep_att = mask_in[1 - s, 0, rows, cols].astype(f32)
+                keep_ff = mask_in[1 - s, 1, rows, cols].astype(f32)
+                total = keep_att * mul(att[c % slots, rows], w_out[s, :, cols])
+                total = total + keep_ff * mul(hid[c % slots, rows], w_down[s, :, cols])
+                merged[s, rows, cols] = total.astype(bf16)
+
+            @pl.when(s == 0)
+            def _():
+                for i in range(2):
+                    branch_copy(4 * c + 2 * h + i).start()
+
+            return carry
+
+        lax.fori_loop(0, 2, one, 0)
+
+    def close(c):
+        finish_joined(c, 1)
 
     from_low = jnp.logical_and(z <= g, z > 0)
     from_high = jnp.logical_and(z >= g, z < n_gx - 1)
     below, above = z < g, z > g
 
     def line_copies(p):
-        c, b = p // 2, p % 2
-        k = p % 4
+        c = p // 4
+        k, rows, held = line_slot(p), piece_rows(p), line_rows(p)
+        own = line_out.at[k, held]
         up = remote(
-            line_out.at[k], line_low.at[k], line_send.at[p], low_recv.at[p], (g, j + sub)
+            own, line_low.at[k, held], line_send.at[p], low_recv.at[p], (g, j + sub)
         )
         down = remote(
-            line_out.at[k],
-            line_high.at[k],
-            line_send.at[p],
-            high_recv.at[p],
-            (g, j - sub),
-        )
-        home = remote(
-            line_out.at[k], final.at[b], line_send.at[p], final_recv.at[b], (c, j)
-        )
+            own, line_high.at[k, held], line_send.at[p], high_recv.at[p], (g, j - sub)
+        )
+        landing = final.at[p // 2 % 2 if c < join else 0, rows]
+        home = remote(own, landing, line_send.at[p], final_recv.at[p % 4], (c, j))
         return up, down, home
 
     def leaves(p):
-        return jnp.logical_not(jnp.logical_and(at_root, g == p // 2))
-
-    def reduce(p):
-        c, b = p // 2, p % 2
-        k = p % 4
+        return jnp.logical_not(jnp.logical_and(at_root, g == p // 4))
+
+    def reduce(n):
+        for p in (2 * n, 2 * n + 1):
+            reduce_piece(p)
+
+    def reduce_piece(p):
+        c = p // 4
+        k, rows = line_slot(p), piece_rows(p)
+        count, offset = rows.stop - rows.start, rows.start
+        shift = line_rows(p).start
         up, down, home = line_copies(p)
         branch_copy(p).wait_recv()
 
-        def begin(rows):
-            running[rows] = branch[c % 2, b, 1, rows].astype(f32) + branch_in[
-                k, rows
+        @pl.when(from_low)
+        def _():
+            up.wait_recv()
+
+        @pl.when(from_high)
+        def _():
+            down.wait_recv()
+
+        if p >= 8:
+
+            @pl.when(leaves(p - 8))
+            def _():
+                line_copies(p - 8)[0].wait_send()
+
+            @pl.when(jnp.logical_not(at_root))
+            def _():
+                pl.semaphore_wait(line_credit, 1)
+
+        def total_rows(step):
+            total = branch_ref(p, 1)[step].astype(f32) + branch_in[
+                piece_slot(p), pl.ds(offset + step.start, ROW_STEP)
             ].astype(f32)
-
-        over_rows(seq, begin)
-        if p < 4:
-            pl.semaphore_signal(
-                branch_credit, inc=1, device_id=side, device_id_type=MESH
-            )
-        for here, copy, held, source in (
-            (from_low, up, line_low, (g, j - sub)),
-            (from_high, down, line_high, (g, j + sub)),
-        ):
-
-            @pl.when(here)
-            def _():
-                copy.wait_recv()
-
-                def add(rows):
-                    running[rows] = running[rows] + held[k, rows].astype(f32)
-
-                over_rows(seq, add)
-                if p < 4:
+            low = line_low[k, pl.ds(shift + step.start, ROW_STEP)].astype(f32)
+            high = line_high[k, pl.ds(shift + step.start, ROW_STEP)].astype(f32)
+            total = total + jnp.where(from_low, low, 0.0)
+            total = total + jnp.where(from_high, high, 0.0)
+            line_out[k, pl.ds(shift + step.start, ROW_STEP)] = total.astype(bf16)
+
+        over_rows(count, total_rows)
+        if p < 8:
+            for here, source in ((from_low, j - sub), (from_high, j + sub)):
+
+                @pl.when(here)
+                def _():
                     pl.semaphore_signal(
-                        line_credit, inc=1, device_id=source, device_id_type=MESH
+                        line_credit, inc=1, device_id=(g, source), device_id_type=MESH
                     )
-
-        if p >= 4:
-
-            @pl.when(leaves(p - 4))
-            def _():
-                line_copies(p - 4)[0].wait_send()
-
-            @pl.when(jnp.logical_not(at_root))
-            def _():
-                pl.semaphore_wait(line_credit, 1)
-
-        def settle(rows):
-            line_out[k, rows] = running[rows].astype(bf16)
-
-        over_rows(seq, settle)
 
         @pl.when(below)
         def _():
@@ -782,60 +1015,104 @@
         def _():
             @pl.when(g == c)
             def _():
-                final[b] = line_out[k]
+                final[p // 2 % 2 if c < join else 0, rows] = line_out[k, line_rows(p)]
 
             @pl.when(g != c)
             def _():
                 home.start()
 
-    gather(0)
-    exchange(0)
-    gather(1)
-    exchange(1)
-    gather(2)
-    gather(3)
-    activate(0)
-    exchange(2)
-    activate(1)
-    forward(0)
-    finish(0)
-    exchange(3)
-    activate(2)
-    reduce(0)
-    reduce(1)
-    forward(1)
-    finish(1)
-    activate(3)
-    reduce(2)
-    reduce(3)
-    forward(2)
-    finish(2)
-    forward(3)
-    finish(3)
-    for p in range(4, 8):
-        reduce(p)
-
-    for copy in keep_copies:
-        copy.wait()
-
-    @pl.when(jnp.logical_not(at_root))
+    steps = dict(
+        relay=gather,
+        gather=gather,
+        masks=masks,
+        mark=mark,
+        exchange=exchange,
+        activate=activate,
+        forward=forward,
+        finish=finish,
+        close=close,
+        reduce=reduce,
+    )
+    hops = jnp.where(at_root, 3, jnp.where(below, z, n_gx - 1 - z))
+    roles = {
+        "relay": duty,
+        "gather": jnp.logical_not(duty),
+        "root": at_root,
+        "mid": jnp.logical_and(duty, jnp.logical_not(at_root)),
+        "near": jnp.logical_and(duty, jnp.abs(z - g) == 1),
+        "far": jnp.logical_and(duty, jnp.abs(z - g) > 1),
+        "end": jnp.logical_not(duty),
+        "late": hops > 0,
+    }
+    for d in range(n_gx):
+        roles[str(d)] = hops == d
+    for act, c, role in schedule():
+        with scope(f"{act}{c}"):
+            step = functools.partial(steps[act], c)
+            if role or act in ("relay", "gather"):
+                pl.when(roles[role or act])(step)
+            else:
+                step()
+
+    def arrive(p):
+        @pl.when(jnp.logical_not(at_root))
+        def _():
+            line_copies(p)[2].wait_recv()
+
+    @pl.when(g < join)
     def _():
         for b in range(2):
-            line_copies(b)[2].wait_recv()
-
-    def last(rows):
-        total = keeps[0, 0, rows].astype(f32) * final[0, rows].astype(f32)
-        total = total + keeps[1, 0, rows].astype(f32) * final[1, rows].astype(f32)
-        result[0, rows] = (tokens[0, rows].astype(f32) + total * keep_scale).astype(
-            bf16
-        )
-
-    over_rows(seq, last)
+            keep_copies[b].wait()
+        for p in range(4):
+            arrive(p)
+
+        def last(rows):
+            total = keeps[0, 0, rows].astype(f32) * final[0, rows].astype(f32)
+            total = total + keeps[1, 0, rows].astype(f32) * final[1, rows].astype(f32)
+            result[0, rows] = (
+                tokens[0, rows].astype(f32) + total * keep_scale
+            ).astype(bf16)
+
+        over_rows(seq, last)
+
+    @pl.when(g >= join)
+    def _():
+        for p in range(4):
+            arrive(4 * join + p)
+
+        def last(rows):
+            total = final[0, rows].astype(f32)
+            result[0, rows] = (
+                tokens[0, rows].astype(f32) + total * keep_scale
+            ).astype(bf16)
+
+        over_rows(seq, last)
+
+        @pl.when(jnp.logical_not(at_root))
+        def _():
+            for i in range(4):
+                mask_first_copy(i).wait_send()
+
+    @pl.when(at_root)
+    def _():
+        for i in range(4):
+            mask_beside(i).wait_send()
+
+    for i in range(8):
+        down, up = mask_copies(i)
+
+        @pl.when(goes_up)
+        def _():
+            up.wait_send()
+
+        @pl.when(goes_down)
+        def _():
+            down.wait_send()
 
     for copy in stat_copies:
         copy.wait_send()
 
-    @pl.when(jnp.logical_not(at_root))
+    @pl.when(jnp.logical_and(jnp.logical_not(at_root), g % 2 == 1))
     def _():
         for copy in first_copies:
             copy.wait_send()
@@ -853,14 +1130,18 @@
             def _():
                 down.wait_send()
 
-        for which in range(2):
-            for copy in share_copies(c, which):
+        for unit in range(3) if c >= chunks - slots else []:
+            for copy in share_copies(c, unit):
                 copy.wait_send()
     for half in range(2):
-        part_copy(chunks - 1, half).wait_send()
+        for section in sections(chunks - 1):
+            part_copy(chunks - 1, half, section).wait_send()
     for c in range(chunks - 2, chunks):
-        cross_copy(c).wait_send()
-    for p in range(4, 8):
+        for section in sections(c):
+            cross_copy(c, section).wait_send()
+    for p in range(8):
+        branch_copy(p).wait_send()
+    for p in range(8, 16):
         branch_copy(p).wait_send()
 
         @pl.when(leaves(p))
@@ -887,7 +1168,7 @@
     head = query_gain.shape[0]
     quarter_head, quarter_ff = head_cols // n_gx, ff_cols // n_gx
     quarter = 3 * quarter_head + quarter_ff
-    chunks, pieces = n_gx, 2 * n_gx
+    chunks, pieces = n_gx, 4 * n_gx
     dma, vmem = pltpu.SemaphoreType.DMA, pltpu.VMEM
     scratch = [
         vmem((n_gx, block_width, quarter), bf16),
@@ -903,15 +1184,17 @@
         vmem((2, seq, quarter), f32),
         vmem((2, seq, quarter), bf16),
         vmem((chunks, seq, quarter), bf16),
-        vmem((chunks, seq, ff_cols), bf16),
-        vmem((chunks, seq, head_cols), bf16),
-        vmem((2, 2, 2, seq, slice_width), bf16),
+        vmem((3, seq, ff_cols), bf16),
+        vmem((3, seq, head_cols), bf16),
+        vmem((3, 2, 2, seq, slice_width), bf16),
+        vmem((2, seq, slice_width), bf16),
+        vmem((7, seq, slice_width), bf16),
         vmem((4, seq, slice_width), bf16),
         vmem((4, seq, slice_width), bf16),
         vmem((4, seq, slice_width), bf16),
-        vmem((4, seq, slice_width), bf16),
-        vmem((seq, slice_width), f32),
         vmem((2, seq, slice_width), bf16),
+        vmem((2, seq, slice_width), bf16),
+        vmem((2, 2, seq, slice_width), bf16),
         dma((n_gx, 8)),
         dma((2, n_gx)),
         dma((2, n_gx)),
@@ -923,18 +1206,22 @@
         dma((2, chunks, GATHER_PIECES)),
         dma((chunks, GATHER_PIECES)),
         dma((chunks, GATHER_PIECES)),
+        dma((chunks, 2, 2)),
+        dma((chunks, 2, 2)),
         dma((chunks, 2)),
         dma((chunks, 2)),
-        dma((chunks,)),
-        dma((chunks,)),
-        dma((chunks, 2, 3)),
-        dma((chunks, 2, 3)),
+        dma((chunks, 3, 3)),
+        dma((chunks, 3, 3)),
         dma((pieces,)),
         dma((pieces,)),
         dma((pieces,)),
         dma((pieces,)),
         dma((pieces,)),
-        dma((2,)),
+        dma((4,)),
+        dma((4,)),
+        dma((8,)),
+        dma((2, 8)),
+        dma((4,)),
         pltpu.SemaphoreType.REGULAR,
         pltpu.SemaphoreType.REGULAR,
     ]

time: 212 us -> 174 us (0.82)
  Pallas kernels: 209 us -> 170 us
    pallas_call x1, Pallas kernels: 209 us -> 170 us  [fused(): pl.pallas_call(functools.partial(block_kernel, n_gy), out_shape=jax.Shape...]
where the time goes in v2:
time: 174 us; the launch traced here: 172 us
  Pallas kernels  170 us (98%)
  local copies, waits for them, and re-layouts  1.77 us (1%)
    pallas_call x1, Pallas kernels, fused(): pl.pallas_call(functools.partial(block_kernel, n_gy), out_shape=jax.Shape...  170 us

profile of v2, /device:TPU:2, one launch (start us, length us, event | category | flops | bytes accessed | tf_op | source)
XLA Modules:
  0.0 171.8 jit_solution(9315026328430921291)
XLA Ops:
  0.0 170.1 %shard_map.100 = bf16[1,256,768]{2,1,0:T(8,128)(2,1)} custom-call(bf16[1,256,768]{2,1,0:T(8,128)(2,1)} %tokens.1, f32[8,1,768]{2,1,0:T(1,128)} %bitcast.5, f32[1,128]{1,0:T(1,128)} %bitcast.6, f32[1,128]{1,0:T(1,128)} %bitcast.7, bf16[3,1536,512]{2,1,0:T(8,128)(2,1)} %bitcast.4, bf16[1536,3072]{1,0:T(8,128)(2,1)} %up_hbm.1, bf16[512,1536]{1,0:T(8,128)(2,1)} %out_hbm.1, ...), custom_call_target="tpu_custom_call" | custom-call | tf_op jit(solution)/shard_map/pallas_call | solution.py:1230
  170.1 1.8 %copy.12 = bf16[1,256,768]{2,1,0:T(8,128)(2,1)} copy(bf16[1,256,768]{2,1,0:T(8,128)(2,1)} %shard_map.100) | data formatting | bytes 786432

commit v3 on v2

--- a/solution.py
+++ b/solution.py
@@ -272,14 +272,14 @@
 
 SCHEDULE = (
     "mark0", "relay0", "relay1", "relay2/root", "relay3/root", "gather0", "exchange0",
-    "relay2/mid", "exchange1", "masks0/root", "relay3/mid", "activate0",
-    "masks1/root", "gather3", "exchange2", "activate1", "masks0/near", "forward0", "finish0",
-    "masks1/near", "reduce0/0", "activate2", "exchange3", "masks0/far", "reduce1/0",
-    "reduce0/1", "forward1", "finish1", "masks1/far", "reduce1/1", "reduce0/2", "forward2",
-    "finish2", "reduce2/0", "reduce3/0", "reduce1/2", "activate3", "reduce2/1", "reduce0/3",
-    "reduce1/3", "reduce4/0", "reduce3/1", "forward3", "masks0/end", "masks1/end",
-    "finish3", "reduce5/0", "close3", "reduce2/2", "reduce3/2", "reduce2/3", "reduce3/3", "reduce4/late",
-    "reduce5/late", "reduce6", "reduce7",
+    "relay2/mid", "exchange1", "masks2/root", "masks0/root", "relay3/mid", "activate0",
+    "masks2/near", "masks1/root", "gather3", "exchange2", "activate1", "masks0/near",
+    "forward0", "finish0", "masks2/far", "masks1/near", "reduce0/0", "activate2", "exchange3",
+    "masks0/far", "reduce1/0", "reduce0/1", "forward1", "finish1", "masks1/far", "reduce1/1",
+    "reduce0/2", "forward2", "finish2", "reduce2/0", "reduce3/0", "reduce1/2", "activate3",
+    "reduce2/1", "reduce0/3", "reduce1/3", "reduce3/1", "reduce2/2", "forward3", "masks2/end",
+    "reduce4/0", "reduce5/0", "masks0/end", "masks1/end", "finish3", "reduce4/1", "close3", "reduce3/2",
+    "reduce2/3", "reduce3/3", "reduce4/2", "reduce4/3", "reduce5/late", "reduce6", "reduce7",
 )
 
 
@@ -549,23 +549,26 @@
 
         pl.semaphore_signal(turn, inc=1, device_id=core, device_id_type=MESH)
 
-    join = chunks - 1
+    join, fuse = chunks - 1, chunks - 2
     half_rows = seq // 2
 
     def mask_ref(i):
         return mask_in.at[i // 4, i // 2 % 2, pl.ds(i % 2 * half_rows, half_rows)]
 
+    mask_slot = 2 * (join - g)
+
     def mask_first_copy(i):
+        part_of = (i // 2, pl.ds(i % 2 * half_rows, half_rows))
         return remote(
-            mask_own.at[i // 2, pl.ds(i % 2 * half_rows, half_rows)],
-            mask_ref(i),
+            mask_own.at[part_of],
+            mask_in.at[(mask_slot, *part_of)],
             mask_first.at[i],
-            mask_recv.at[i],
+            mask_recv.at[4 * mask_slot + i],
             (z, j),
         )
 
     def mark(_):
-        @pl.when(g >= join)
+        @pl.when(g >= fuse)
         def _():
             for b in range(2):
                 keep_copies[b].wait()
@@ -577,7 +580,7 @@
 
             @pl.when(at_root)
             def _():
-                mask_in[0] = mask_own[...]
+                mask_in[mask_slot] = mask_own[...]
 
             @pl.when(jnp.logical_not(at_root))
             def _():
@@ -602,18 +605,20 @@
     def masks(s):
         for i in range(4 * s, 4 * s + 4):
             down, up = mask_copies(i)
-            if s == 0:
-
-                @pl.when(jnp.logical_not(jnp.logical_and(at_root, g == join)))
+            if s == 1:
+                up.wait_recv()
+            else:
+                image = join if s == 0 else fuse
+
+                @pl.when(jnp.logical_not(jnp.logical_and(at_root, g == image)))
                 def _():
                     up.wait_recv()
+
+            if s == 0:
 
                 @pl.when(at_root)
                 def _():
                     mask_beside(i).start()
-
-            else:
-                up.wait_recv()
 
             @pl.when(goes_up)
             def _():
@@ -855,8 +860,13 @@
     def line_slot(p):
         return p // 2 % 4
 
+    def sum_rows(p):
+        if p // 4 < fuse:
+            return piece_rows(p)
+        return slice(p % 4 * quarter_rows, (p % 4 + 1) * quarter_rows)
+
     def line_rows(p):
-        rows = piece_rows(p)
+        rows = sum_rows(p)
         start = p % 2 * half_rows
         return slice(start, start + rows.stop - rows.start)
 
@@ -938,7 +948,7 @@
 
     def line_copies(p):
         c = p // 4
-        k, rows, held = line_slot(p), piece_rows(p), line_rows(p)
+        k, rows, held = line_slot(p), sum_rows(p), line_rows(p)
         own = line_out.at[k, held]
         up = remote(
             own, line_low.at[k, held], line_send.at[p], low_recv.at[p], (g, j + sub)
@@ -946,7 +956,7 @@
         down = remote(
             own, line_high.at[k, held], line_send.at[p], high_recv.at[p], (g, j - sub)
         )
-        landing = final.at[p // 2 % 2 if c < join else 0, rows]
+        landing = final.at[p // 2 % 2 if c < fuse else 0, rows]
         home = remote(own, landing, line_send.at[p], final_recv.at[p % 4], (c, j))
         return up, down, home
 
@@ -959,11 +969,15 @@
 
     def reduce_piece(p):
         c = p // 4
-        k, rows = line_slot(p), piece_rows(p)
+        k, rows = line_slot(p), sum_rows(p)
         count, offset = rows.stop - rows.start, rows.start
         shift = line_rows(p).start
         up, down, home = line_copies(p)
-        branch_copy(p).wait_recv()
+        if c < fuse or c >= join:
+            branch_copy(p).wait_recv()
+        elif p % 2 == 0:
+            for b in range(2):
+                branch_copy(4 * c + 2 * b + p // 2 % 2).wait_recv()
 
         @pl.when(from_low)
         def _():
@@ -984,9 +998,18 @@
                 pl.semaphore_wait(line_credit, 1)
 
         def total_rows(step):
-            total = branch_ref(p, 1)[step].astype(f32) + branch_in[
-                piece_slot(p), pl.ds(offset + step.start, ROW_STEP)
-            ].astype(f32)
+            here = pl.ds(offset + step.start, ROW_STEP)
+            if c < fuse or c >= join:
+                total = branch_ref(p, 1)[step].astype(f32) + branch_in[
+                    piece_slot(p), here
+                ].astype(f32)
+            else:
+                total = 0.0
+                for b in range(2):
+                    both = branch[c, b, 1, here].astype(f32) + branch_in[
+                        2 * c + b, here
+                    ].astype(f32)
+                    total = total + mask_in[2, b, here].astype(f32) * both
             low = line_low[k, pl.ds(shift + step.start, ROW_STEP)].astype(f32)
             high = line_high[k, pl.ds(shift + step.start, ROW_STEP)].astype(f32)
             total = total + jnp.where(from_low, low, 0.0)
@@ -1015,7 +1038,7 @@
         def _():
             @pl.when(g == c)
             def _():
-                final[p // 2 % 2 if c < join else 0, rows] = line_out[k, line_rows(p)]
+                final[p // 2 % 2 if c < fuse else 0, rows] = line_out[k, line_rows(p)]
 
             @pl.when(g != c)
             def _():
@@ -1059,7 +1082,7 @@
         def _():
             line_copies(p)[2].wait_recv()
 
-    @pl.when(g < join)
+    @pl.when(g < fuse)
     def _():
         for b in range(2):
             keep_copies[b].wait()
@@ -1075,7 +1098,7 @@
 
         over_rows(seq, last)
 
-    @pl.when(g >= join)
+    @pl.when(g >= fuse)
     def _():
         for p in range(4):
             arrive(4 * join + p)
@@ -1098,7 +1121,7 @@
         for i in range(4):
             mask_beside(i).wait_send()
 
-    for i in range(8):
+    for i in range(12):
         down, up = mask_copies(i)
 
         @pl.when(goes_up)
@@ -1194,7 +1217,7 @@
         vmem((4, seq, slice_width), bf16),
         vmem((2, seq, slice_width), bf16),
         vmem((2, seq, slice_width), bf16),
-        vmem((2, 2, seq, slice_width), bf16),
+        vmem((3, 2, seq, slice_width), bf16),
         dma((n_gx, 8)),
         dma((2, n_gx)),
         dma((2, n_gx)),
@@ -1219,8 +1242,8 @@
         dma((pieces,)),
         dma((4,)),
         dma((4,)),
-        dma((8,)),
-        dma((2, 8)),
+        dma((12,)),
+        dma((2, 12)),
         dma((4,)),
         pltpu.SemaphoreType.REGULAR,
         pltpu.SemaphoreType.REGULAR,

time: 174 us -> 166 us (0.954)
  Pallas kernels: 170 us -> 162 us
    pallas_call x1, Pallas kernels: 170 us -> 162 us  [fused(): pl.pallas_call(functools.partial(block_kernel, n_gy), out_shape=jax.Shape...]
where the time goes in v3:
time: 166 us; the launch traced here: 164 us
  Pallas kernels  162 us (98%)
  local copies, waits for them, and re-layouts  1.77 us (1%)
    pallas_call x1, Pallas kernels, fused(): pl.pallas_call(functools.partial(block_kernel, n_gy), out_shape=jax.Shape...  162 us

profile of v3, /device:TPU:2, one launch (start us, length us, event | category | flops | bytes accessed | tf_op | source)
XLA Modules:
  0.0 164.2 jit_solution(14252970277769442570)
XLA Ops:
  0.0 162.4 %shard_map.100 = bf16[1,256,768]{2,1,0:T(8,128)(2,1)} custom-call(bf16[1,256,768]{2,1,0:T(8,128)(2,1)} %tokens.1, f32[8,1,768]{2,1,0:T(1,128)} %bitcast.5, f32[1,128]{1,0:T(1,128)} %bitcast.6, f32[1,128]{1,0:T(1,128)} %bitcast.7, bf16[3,1536,512]{2,1,0:T(8,128)(2,1)} %bitcast.4, bf16[1536,3072]{1,0:T(8,128)(2,1)} %up_hbm.1, bf16[512,1536]{1,0:T(8,128)(2,1)} %out_hbm.1, ...), custom_call_target="tpu_custom_call" | custom-call | tf_op jit(solution)/shard_map/pallas_call | solution.py:1253
  162.4 1.8 %copy.12 = bf16[1,256,768]{2,1,0:T(8,128)(2,1)} copy(bf16[1,256,768]{2,1,0:T(8,128)(2,1)} %shard_map.100) | data formatting | bytes 786432
